TPU v7x, 32 devices: a whole 2x2x4 slice. The times are simulated.
32 devices in a mesh: blk: 16 (over z, y, x), rep: 2 (over core).
Axes of the slice: x: 2, y: 2, z: 4, core: 2. Of those that a mesh axis runs over, the one named last changes fastest.
Arguments:
- fwd_in: bfloat16 [14336, 1024], P(('blk', 'rep')), may hold values from -6 to 6
- bwd_in: bfloat16 [14336, 1024], P(('blk', 'rep')), may hold values from -6 to 6
- cotangent: bfloat16 [14336, 1024], P(('blk', 'rep')), may hold values from -6 to 6
- w_in: bfloat16 [1024, 8192], P(None, 'blk'), may hold values from -0.1875 to 0.1875
- w_out: bfloat16 [8192, 1024], P('blk'), may hold values from -0.125 to 0.125
Outputs:
- forward_out: bfloat16 [14336, 1024], P(('blk', 'rep'))
- input_grad: bfloat16 [14336, 1024], P(('blk', 'rep'))
- in_grad: float32 [1024, 8192], P('rep', 'blk')
- down_grad: float32 [8192, 1024], P('blk', 'rep')
All inputs are finite; a program needn't handle non-finite values.
Results may differ from a plain program's by a relative error of at most 0.0066.
Values may be sent and summed in bfloat16 or wider, within the bound.
No kernel may reach another device: no remote copies, remote signals or barrier semaphores. Data moves between devices by JAX's collectives and lax.ppermute only.
A program may use at most 128 MiB of HBM per device.

v0:
```python
import functools

import jax
import jax.numpy as jnp
from jax import lax
from jax.experimental import pallas as pl
from jax.experimental.pallas import tpu as pltpu
from jax.sharding import PartitionSpec as P


TICKS = 4
SIDE = 2
ROOT = 0.7978845608028654
CUBE = 0.044715
F32, BF16 = jnp.float32, jnp.bfloat16


def routes(n_blk, n_rep):
    groups = n_blk // TICKS
    across, beside, returned, forward, third = [], [], [], [], []
    for blk in range(n_blk):
        group, place = blk // TICKS, blk % TICKS
        for rep in range(n_rep):
            source = blk * n_rep + rep

            def target(to):
                to_group = group + (1 if to < place else 0)
                return ((to_group % groups) * TICKS + to) * n_rep + rep

            returned.append((target(place ^ 1), source))
            if place < TICKS - 1:
                beside.append((source, target(place ^ 1)))
            if place == 0:
                third.append((source, (group * TICKS + SIDE) * n_rep + rep))
            across.append((source, target(place ^ SIDE)))
            forward.append((source, (group * TICKS + (place ^ 1)) * n_rep + rep))
    return beside, returned, across, forward, third


def back(pairs):
    return [(target, source) for source, target in pairs]


def mul(left, right, left_dim, right_dim):
    return lax.dot_general(
        left, right, (((left_dim,), (right_dim,)), ((), ())), preferred_element_type=F32
    )


def tanh_part(v):
    return jnp.tanh(ROOT * (v + CUBE * (v * v * v)))


def cut_kernel(dim, whole, part, sem):
    size = part.shape[dim]
    where = pl.ds(pl.multiple_of(lax.axis_index("rep") * size, size), size)
    copy = pltpu.make_async_copy(whole.at[:, where] if dim else whole.at[where, :], part, sem)
    copy.start()
    copy.wait()


def in_kernel(b0, b1, c0, c1, wi, down, slope, hid):
    for half, b in enumerate((b0, b1)):
        v = mul(b[...], wi[...], 1, 0)
        t = tanh_part(v)
        up = 0.5 * (1.0 + t)
        hid[half] = (v * up).astype(BF16)
        slope[half] = up + (0.5 * ROOT) * v * (1.0 - t * t) * (1.0 + (3.0 * CUBE) * (v * v))
    down[...] = (mul(hid[0], c0[...], 0, 0) + mul(hid[1], c1[...], 0, 0)).astype(down.dtype)


def out_kernel(b0, b1, c0, c1, wo, slope, into, pre):
    for half, c in enumerate((c0, c1)):
        pre[half] = (mul(c[...], wo[...], 1, 1) * slope[half]).astype(BF16)
    into[...] = (mul(pre[0], b0[...], 0, 0) + mul(pre[1], b1[...], 0, 0)).astype(into.dtype)


def fwd_kernel(f0, f1, wi, hid):
    for half, f in enumerate((f0, f1)):
        v = mul(f[...], wi[...], 1, 0)
        hid[half] = (v * (0.5 * (1.0 + tanh_part(v)))).astype(BF16)


def sum_kernel(dim, *refs):
    lefts, rights = refs[:TICKS], refs[TICKS : 2 * TICKS]
    give, keep, left, right = refs[2 * TICKS :]
    size = lefts[0].shape[2]
    for slot in range(TICKS):
        where = slice(slot * size, (slot + 1) * size)
        if dim:
            right[:, where] = rights[slot][...]
        else:
            right[where, :] = rights[slot][...]
        for half in range(2):
            left[half, :, where] = lefts[slot][half]
    give[...] = mul(left[1], right[...], 1, dim).astype(BF16)
    keep[...] = mul(left[0], right[...], 1, dim)


def add_kernel(a, b, out):
    out[...] = (a[...].astype(F32) + b[...].astype(F32)).astype(out.dtype)


def split_kernel(own, x, y, keep, give):
    rep, size = lax.axis_index("rep"), keep.shape[1]
    for out, at in ((give, 1 - rep), (keep, rep)):
        where = pl.ds(pl.multiple_of(at * size, size), size)
        out[...] = own[:, where] + x[:, where].astype(F32) + y[:, where].astype(F32)


def join_kernel(dim, keep, got, out):
    rep, size = lax.axis_index("rep"), keep.shape[0]
    for part, at in ((keep, rep), (got, 1 - rep)):
        where = pl.ds(pl.multiple_of(at * size, size), size)
        if dim:
            out[:, where] = part[...].T
        else:
            out[where, :] = part[...]


def call(body, outs, flops, *args, scratch=(), far=False):
    vmem = pl.BlockSpec(memory_space=pltpu.VMEM)
    moved = sum(a.size * a.dtype.itemsize for a in args)
    return pl.pallas_call(
        body,
        out_shape=outs,
        in_specs=[pl.BlockSpec(memory_space=pltpu.HBM) if far else vmem] * len(args),
        out_specs=jax.tree.map(lambda _: vmem, outs),
        scratch_shapes=list(scratch),
        compiler_params=pltpu.CompilerParams(vmem_limit_bytes=14 << 20),
        cost_estimate=pl.CostEstimate(flops=flops, bytes_accessed=moved, transcendentals=0),
    )(*args)


def window(fwd_in, bwd_in, cotangent, w_in, w_out):
    axes = ("blk", "rep")
    n_blk, n_rep = lax.axis_size("blk"), lax.axis_size("rep")
    beside, returned, across, forward, third = routes(n_blk, n_rep)
    width = w_in.shape[1] // n_rep
    rows, model = fwd_in.shape
    span = model // n_rep
    swap = [(0, 1), (1, 0)]
    unit = 2 * 2 * rows * model * width

    def move(value, pairs):
        return lax.ppermute(value, axes, pairs)

    def peer(value):
        return lax.ppermute(value, "rep", swap)

    shape = jax.ShapeDtypeStruct
    hidden = shape((2, rows, width), BF16)

    def run(body, outs, flops, *args, **rest):
        return call(body, outs, flops, *args, **rest)

    def in_part(a, kind):
        return run(
            in_kernel,
            (shape((width, model), kind), shape((2, rows, width), F32)),
            2 * unit,
            bwd_in, bwd_peer, cotangent, cot_peer, a,
            scratch=[pltpu.VMEM((2, rows, width), BF16)],
        )

    def out_part(b, slope, kind):
        return run(
            out_kernel,
            (shape((width, model), kind), hidden),
            2 * unit,
            bwd_in, bwd_peer, cotangent, cot_peer, b, slope,
        )

    def fwd_part(a):
        return run(fwd_kernel, hidden, unit, fwd_in, fwd_peer, a)

    def cut(whole, dim):
        size = (model, width) if dim else (width, model)
        return run(
            functools.partial(cut_kernel, dim), shape(size, BF16), unit // 4, whole,
            scratch=[pltpu.SemaphoreType.DMA], far=True,
        )

    def add(a, b):
        return run(add_kernel, shape(a.shape, BF16), unit // 4, a, b)

    wi, wo = cut(w_in, 1), cut(w_out, 0)
    yi, xi = move(wi, across), move(wi, beside)
    yo, xo = move(wo, across), move(wo, beside)
    bwd_peer, cot_peer, fwd_peer = peer(bwd_in), peer(cotangent), peer(fwd_in)
    di, do = move(yi, forward), move(yo, forward)
    xi = add(xi, move(di, third))
    xo = add(xo, move(do, third))

    down_0, slope_0 = in_part(wi, F32)
    into_0, pre_0 = out_part(wo, slope_0, F32)
    hid_0 = fwd_part(wi)
    down_y, slope_y = in_part(yi, BF16)
    into_y, pre_y = out_part(yo, slope_y, BF16)
    hid_y = fwd_part(yi)
    down_d, slope_d = in_part(di, BF16)
    into_d, pre_d = out_part(do, slope_d, BF16)
    hid_d = fwd_part(di)
    down_x, slope_x = in_part(xi, BF16)
    into_x, pre_x = out_part(xo, slope_x, BF16)
    hid_x = fwd_part(xi)

    down_y = add(down_y, move(down_d, back(forward)))
    into_y = add(into_y, move(into_d, back(forward)))
    down_across, into_across = move(down_y, back(across)), move(into_y, back(across))
    down_beside, into_beside = move(down_x, returned), move(into_x, returned)

    def sums(lefts, rights, dim):
        give, keep = run(
            functools.partial(sum_kernel, dim),
            (shape((rows, model), BF16), shape((rows, model), F32)),
            4 * unit, *lefts, *rights,
            scratch=[
                pltpu.VMEM((2, rows, TICKS * width), BF16),
                pltpu.VMEM((model, TICKS * width) if dim else (TICKS * width, model), BF16),
            ],
        )
        return add(keep, peer(give))

    forward_out = sums((hid_0, hid_x, hid_y, hid_d), (wo, xo, yo, do), 0)
    input_grad = sums((pre_0, pre_x, pre_y, pre_d), (wi, xi, yi, di), 1)

    def share(own, x, y, dim):
        half = shape((width, span), F32)
        keep, give = run(split_kernel, (half, half), unit // 4, own, x, y)
        size = (span, n_rep * width) if dim else (n_rep * width, span)
        return run(
            functools.partial(join_kernel, dim), shape(size, F32), unit // 4,
            keep, peer(give),
        )

    down_grad = share(down_0, down_beside, down_across, 0)
    in_grad = share(into_0, into_beside, into_across, 1)
    return (forward_out, input_grad, in_grad, down_grad)


def solution(mesh):
    in_specs = (
        P(("blk", "rep"), None),
        P(("blk", "rep"), None),
        P(("blk", "rep"), None),
        P(None, "blk"),
        P("blk", None),
    )
    out_specs = (P(("blk", "rep"), None), P(("blk", "rep"), None), P("rep", "blk"), P("blk", "rep"))
    return jax.shard_map(window, mesh=mesh, in_specs=in_specs, out_specs=out_specs, check_vma=False)
```

profile of v0, /device:TPU:0, one launch (start us, length us, event | category | flops | bytes accessed | tf_op | source)
XLA Modules:
  0.0 136.0 jit_solution(10303215279661128739)
XLA Ops:
  0.7 1.3 copy-done.3
  2.1 3.0 %collective-permute-start.2 = (bf16[1024,256]{1,0:T(8,128)(2,1)S(1)}, bf16[1024,256]{1,0:T(8,128)(2,1)S(1)}, u32[]{:S(2)}, u32[]{:S(2)}) collective-permute-start(bf16[1024,256]{1,0:T(8,128)(2,1)S(1)} %shard_map.84.wi.refs_4_), channel_id=1, source_target_pairs={{0,4},{1,5},{2,6},{3,7},{4,8},{5,9},{6,10},{7,11},{8,12},{9,13},{1... | collective-permute-start | bytes 1572872 | tf_op jit(solution)/shard_map/ppermute | solution.py:146
  5.1 0.5 collective-permute-start.11
  5.6 1.2 copy-done.4
  6.9 1.6 %collective-permute-start.6 = (bf16[256,1024]{1,0:T(8,128)(2,1)S(1)}, bf16[256,1024]{1,0:T(8,128)(2,1)S(1)}, u32[]{:S(2)}, u32[]{:S(2)}) collective-permute-start(bf16[256,1024]{1,0:T(8,128)(2,1)S(1)} %shard_map.90.refs_4_.wo), channel_id=1, source_target_pairs={{0,4},{1,5},{2,6},{3,7},{4,8},{5,9},{6,10},{7,11},{8,12},{9,13},{1... | collective-permute-start | bytes 1572872 | tf_op jit(solution)/shard_map/ppermute | solution.py:146
  8.5 12.4 %collective-permute-done.2.wi.refs_6_ = bf16[1024,256]{1,0:T(8,128)(2,1)S(1)} collective-permute-done((bf16[1024,256]{1,0:T(8,128)(2,1)S(1)}, bf16[1024,256]{1,0:T(8,128)(2,1)S(1)}, u32[]{:S(2)}, u32[]{:S(2)}) %collective-permute-start.2) | collective-permute-done | bytes 524320 | tf_op jit(solution)/shard_map/ppermute | solution.py:146
  20.9 1.7 %collective-permute-start.3 = (bf16[1024,256]{1,0:T(8,128)(2,1)S(1)}, bf16[1024,256]{1,0:T(8,128)(2,1)S(1)}, u32[]{:S(2)}, u32[]{:S(2)}) collective-permute-start(bf16[1024,256]{1,0:T(8,128)(2,1)S(1)} %collective-permute-done.2.wi.refs_6_), channel_id=1, source_target_pairs={{0,2},{1,3},{2,0},{3,1},{4,6},{5,7},{6,4},{7,5},{8,10},{9,11},{10,... | collective-permute-start | bytes 1572872 | tf_op jit(solution)/shard_map/ppermute | solution.py:146
  22.6 8.7 %collective-permute-done.6.refs_6_.wo = bf16[256,1024]{1,0:T(8,128)(2,1)S(1)} collective-permute-done((bf16[256,1024]{1,0:T(8,128)(2,1)S(1)}, bf16[256,1024]{1,0:T(8,128)(2,1)S(1)}, u32[]{:S(2)}, u32[]{:S(2)}) %collective-permute-start.6) | collective-permute-done | bytes 524320 | tf_op jit(solution)/shard_map/ppermute | solution.py:146
  31.3 1.5 %collective-permute-start.7 = (bf16[256,1024]{1,0:T(8,128)(2,1)S(1)}, bf16[256,1024]{1,0:T(8,128)(2,1)S(1)}, u32[]{:S(2)}, u32[]{:S(2)}) collective-permute-start(bf16[256,1024]{1,0:T(8,128)(2,1)S(1)} %collective-permute-done.6.refs_6_.wo), channel_id=1, source_target_pairs={{0,2},{1,3},{2,0},{3,1},{4,6},{5,7},{6,4},{7,5},{8,10},{9,11},{10,... | collective-permute-start | bytes 1572872 | tf_op jit(solution)/shard_map/ppermute | solution.py:146
  32.8 0.4 collective-permute-done.3.wi.refs_7_
  33.2 1.7 %shard_map.100 = (bf16[256,1024]{1,0:T(8,128)(2,1)S(1)}, f32[2,448,256]{2,1,0:T(8,128)S(1)}) custom-call(bf16[448,1024]{1,0:T(8,128)(2,1)S(1)} %copy-done, bf16[448,1024]{1,0:T(8,128)(2,1)S(1)} %collective-permute-done.10.b1, bf16[448,1024]{1,0:T(8,128)(2,1)S(1)} %copy-done.1, bf16[448,1024]{1,0:T(8,128)(2,1)S(1)} %collective-permute-done.11.c1, ...), custom_call_target="tpu_custom_call" | custom-call | flops 939524096 | bytes 4194304 | tf_op jit(solution)/shard_map/pallas_call | solution.py:124
  34.9 1.4 %collective-permute-start.18 = (bf16[256,1024]{1,0:T(8,128)(2,1)S(1)}, bf16[256,1024]{1,0:T(8,128)(2,1)S(1)}, u32[]{:S(2)}, u32[]{:S(2)}) collective-permute-start(bf16[256,1024]{1,0:T(8,128)(2,1)S(1)} %get-tuple-element.49), channel_id=1, source_target_pairs={{2,0},{3,1},{0,2},{1,3},{6,4},{7,5},{4,6},{5,7},{10,8},{11,9},{8,1... | collective-permute-start | bytes 1572872 | tf_op jit(solution)/shard_map/ppermute | solution.py:146
  36.3 2.6 %collective-permute-start.1 = (bf16[1024,256]{1,0:T(8,128)(2,1)S(1)}, bf16[1024,256]{1,0:T(8,128)(2,1)S(1)}, u32[]{:S(2)}, u32[]{:S(2)}) collective-permute-start(bf16[1024,256]{1,0:T(8,128)(2,1)S(1)} %shard_map.84.wi.refs_4_), channel_id=1, source_target_pairs={{0,2},{1,3},{2,8},{3,9},{4,6},{5,7},{8,10},{9,11},{10,16},{11,17},... | collective-permute-start | bytes 1572872 | tf_op jit(solution)/shard_map/ppermute | solution.py:146
  38.9 2.2 %collective-permute-start.5 = (bf16[256,1024]{1,0:T(8,128)(2,1)S(1)}, bf16[256,1024]{1,0:T(8,128)(2,1)S(1)}, u32[]{:S(2)}, u32[]{:S(2)}) collective-permute-start(bf16[256,1024]{1,0:T(8,128)(2,1)S(1)} %shard_map.90.refs_4_.wo), channel_id=1, source_target_pairs={{0,2},{1,3},{2,8},{3,9},{4,6},{5,7},{8,10},{9,11},{10,16},{11,17},... | collective-permute-start | bytes 1572872 | tf_op jit(solution)/shard_map/ppermute | solution.py:146
  41.1 0.8 shard_map.88.refs_2_
  41.9 1.3 collective-permute-start.4
  43.2 25.3 %collective-permute-done.7.refs_7_.wo = bf16[256,1024]{1,0:T(8,128)(2,1)S(1)} collective-permute-done((bf16[256,1024]{1,0:T(8,128)(2,1)S(1)}, bf16[256,1024]{1,0:T(8,128)(2,1)S(1)}, u32[]{:S(2)}, u32[]{:S(2)}) %collective-permute-start.7) | collective-permute-done | bytes 524320 | tf_op jit(solution)/shard_map/ppermute | solution.py:146
  68.6 1.3 shard_map.101
  70.0 9.8 %collective-permute-done.18.b = bf16[256,1024]{1,0:T(8,128)(2,1)S(1)} collective-permute-done((bf16[256,1024]{1,0:T(8,128)(2,1)S(1)}, bf16[256,1024]{1,0:T(8,128)(2,1)S(1)}, u32[]{:S(2)}, u32[]{:S(2)}) %collective-permute-start.18) | collective-permute-done | bytes 524320 | tf_op jit(solution)/shard_map/ppermute | solution.py:146
  79.8 1.3 collective-permute-start.8
  81.1 0.8 shard_map.85.refs_0_
  82.0 1.7 %shard_map.98 = (bf16[256,1024]{1,0:T(8,128)(2,1)S(1)}, f32[2,448,256]{2,1,0:T(8,128)S(1)}) custom-call(bf16[448,1024]{1,0:T(8,128)(2,1)S(1)} %copy-done, bf16[448,1024]{1,0:T(8,128)(2,1)S(1)} %collective-permute-done.10.b1, bf16[448,1024]{1,0:T(8,128)(2,1)S(1)} %copy-done.1, bf16[448,1024]{1,0:T(8,128)(2,1)S(1)} %collective-permute-done.11.c1, ...), custom_call_target="tpu_custom_call" | custom-call | flops 939524096 | bytes 4194304 | tf_op jit(solution)/shard_map/pallas_call | solution.py:124
  83.6 1.7 %shard_map.94 = (f32[256,1024]{1,0:T(8,128)S(1)}, f32[2,448,256]{2,1,0:T(8,128)S(1)}) custom-call(bf16[448,1024]{1,0:T(8,128)(2,1)S(1)} %copy-done, bf16[448,1024]{1,0:T(8,128)(2,1)S(1)} %collective-permute-done.10.b1, bf16[448,1024]{1,0:T(8,128)(2,1)S(1)} %copy-done.1, bf16[448,1024]{1,0:T(8,128)(2,1)S(1)} %collective-permute-done.11.c1, ...), custom_call_target="tpu_custom_call" | custom-call | flops 939524096 | bytes 4194304 | tf_op jit(solution)/shard_map/pallas_call | solution.py:124
  85.3 1.3 shard_map.99
  86.7 1.3 shard_map.95
  88.0 0.8 shard_map.89.refs_3_
  88.8 0.1 shard_map.107
  89.0 0.2 collective-permute-start.19
  89.2 0.1 shard_map.86.wi.refs_5_
  89.4 1.7 %shard_map.96 = (bf16[256,1024]{1,0:T(8,128)(2,1)S(1)}, f32[2,448,256]{2,1,0:T(8,128)S(1)}) custom-call(bf16[448,1024]{1,0:T(8,128)(2,1)S(1)} %copy-done, bf16[448,1024]{1,0:T(8,128)(2,1)S(1)} %collective-permute-done.10.b1, bf16[448,1024]{1,0:T(8,128)(2,1)S(1)} %copy-done.1, bf16[448,1024]{1,0:T(8,128)(2,1)S(1)} %collective-permute-done.11.c1, ...), custom_call_target="tpu_custom_call" | custom-call | flops 939524096 | bytes 4194304 | tf_op jit(solution)/shard_map/pallas_call | solution.py:124
  91.1 0.1 shard_map.104
  91.3 3.2 %collective-permute-start.15 = (bf16[256,1024]{1,0:T(8,128)(2,1)S(1)}, bf16[256,1024]{1,0:T(8,128)(2,1)S(1)}, u32[]{:S(2)}, u32[]{:S(2)}) collective-permute-start(bf16[256,1024]{1,0:T(8,128)(2,1)S(1)} %shard_map.104), channel_id=1, source_target_pairs={{4,0},{5,1},{6,2},{7,3},{8,4},{9,5},{10,6},{11,7},{12,8},{13,9},{1... | collective-permute-start | bytes 1572872 | tf_op jit(solution)/shard_map/ppermute | solution.py:146
  94.4 6.1 %collective-permute-done.8.b = bf16[256,1024]{1,0:T(8,128)(2,1)S(1)} collective-permute-done((bf16[256,1024]{1,0:T(8,128)(2,1)S(1)}, bf16[256,1024]{1,0:T(8,128)(2,1)S(1)}, u32[]{:S(2)}, u32[]{:S(2)}) %collective-permute-start.8) | collective-permute-done | bytes 524320 | tf_op jit(solution)/shard_map/ppermute | solution.py:146
  100.5 0.1 shard_map.91.refs_5_.wo
  100.6 1.3 shard_map.97
  102.0 2.1 %shard_map.102 = (bf16[448,1024]{1,0:T(8,128)(2,1)S(1)}, f32[448,1024]{1,0:T(8,128)S(1)}) custom-call(bf16[2,448,256]{2,1,0:T(8,128)(2,1)S(1)} %get-tuple-element.31.refs_0_, bf16[2,448,256]{2,1,0:T(8,128)(2,1)S(1)} %get-tuple-element.33.refs_1_, bf16[2,448,256]{2,1,0:T(8,128)(2,1)S(1)} %get-tuple-element.35.refs_2_, ...), custom_call_target="tpu_custom_call" | custom-call | flops 1879048192 | bytes 3932160 | tf_op jit(solution)/shard_map/pallas_call | solution.py:124
  104.2 0.8 shard_map.87.refs_1_
  105.0 2.1 %shard_map.92 = (bf16[448,1024]{1,0:T(8,128)(2,1)S(1)}, f32[448,1024]{1,0:T(8,128)S(1)}) custom-call(bf16[2,448,256]{2,1,0:T(8,128)(2,1)S(1)} %shard_map.85.refs_0_, bf16[2,448,256]{2,1,0:T(8,128)(2,1)S(1)} %shard_map.87.refs_1_, bf16[2,448,256]{2,1,0:T(8,128)(2,1)S(1)} %shard_map.88.refs_2_, bf16[2,448,256]{2,1,0:T(8,128)(2,1)S(1)} %shard_map.89.refs_3_, ...), custom_call_target="tpu_custom_call" | custom-call | flops 1879048192 | bytes 3932160 | tf_op jit(solution)/shard_map/pallas_call | solution.py:124
  107.1 0.5 collective-permute-start.9
  107.7 5.1 %collective-permute-done.17.x = bf16[256,1024]{1,0:T(8,128)(2,1)S(1)} collective-permute-done((bf16[256,1024]{1,0:T(8,128)(2,1)S(1)}, bf16[256,1024]{1,0:T(8,128)(2,1)S(1)}, u32[]{:S(2)}, u32[]{:S(2)}) %collective-permute-start.17) | collective-permute-done | bytes 524320 | tf_op jit(solution)/shard_map/ppermute | solution.py:146
  112.8 0.2 shard_map.108
  113.0 11.0 %collective-permute-done.15.y = bf16[256,1024]{1,0:T(8,128)(2,1)S(1)} collective-permute-done((bf16[256,1024]{1,0:T(8,128)(2,1)S(1)}, bf16[256,1024]{1,0:T(8,128)(2,1)S(1)}, u32[]{:S(2)}, u32[]{:S(2)}) %collective-permute-start.15) | collective-permute-done | bytes 524320 | tf_op jit(solution)/shard_map/ppermute | solution.py:146
  124.0 7.2 %collective-permute-done.13.x = bf16[256,1024]{1,0:T(8,128)(2,1)S(1)} collective-permute-done((bf16[256,1024]{1,0:T(8,128)(2,1)S(1)}, bf16[256,1024]{1,0:T(8,128)(2,1)S(1)}, u32[]{:S(2)}, u32[]{:S(2)}) %collective-permute-start.13) | collective-permute-done | bytes 524320 | tf_op jit(solution)/shard_map/ppermute | solution.py:146
  131.3 0.2 shard_map.105
  131.5 1.1 shard_map.103
  132.6 1.1 shard_map.93
  133.7 1.0 shard_map.109
  134.7 1.3 shard_map.106
  (30 shorter events, 0.6 us)
Async XLA Ops:
  0.6 32.5 %copy-start = (bf16[448,1024]{1,0:T(8,128)(2,1)S(1)}, bf16[448,1024]{1,0:T(8,128)(2,1)}, u32[]{:S(2)}) copy-start(bf16[448,1024]{1,0:T(8,128)(2,1)} %b0.15) | copy-start | bytes 2752516
  0.6 32.5 %copy-start.1 = (bf16[448,1024]{1,0:T(8,128)(2,1)S(1)}, bf16[448,1024]{1,0:T(8,128)(2,1)}, u32[]{:S(2)}) copy-start(bf16[448,1024]{1,0:T(8,128)(2,1)} %c0.15) | copy-start | bytes 2752516
  0.7 1.4 copy-start.3
  2.0 20.6 %copy-start.2 = (bf16[448,1024]{1,0:T(8,128)(2,1)S(1)}, bf16[448,1024]{1,0:T(8,128)(2,1)}, u32[]{:S(2)}) copy-start(bf16[448,1024]{1,0:T(8,128)(2,1)} %f0.7) | copy-start | bytes 2752516
  2.1 18.9 %collective-permute-start.2 = (bf16[1024,256]{1,0:T(8,128)(2,1)S(1)}, bf16[1024,256]{1,0:T(8,128)(2,1)S(1)}, u32[]{:S(2)}, u32[]{:S(2)}) collective-permute-start(bf16[1024,256]{1,0:T(8,128)(2,1)S(1)} %shard_map.84.wi.refs_4_), channel_id=1, source_target_pairs={{0,4},{1,5},{2,6},{3,7},{4,8},{5,9},{6,10},{7,11},{8,12},{9,13},{1... | collective-permute-start | bytes 1572872 | tf_op jit(solution)/shard_map/ppermute | solution.py:146
  5.1 27.7 %collective-permute-start.10 = (bf16[448,1024]{1,0:T(8,128)(2,1)}, bf16[448,1024]{1,0:T(8,128)(2,1)S(1)}, u32[]{:S(2)}, u32[]{:S(2)}) collective-permute-start(bf16[448,1024]{1,0:T(8,128)(2,1)} %b0.15), channel_id=1, source_target_pairs={{0,1},{1,0},{2,3},{3,2},{4,5},{5,4},{6,7},{7,6},{8,9},{9,8},{10,11... | collective-permute-start | bytes 2752520 | tf_op jit(solution)/shard_map/ppermute | solution.py:149
  5.1 27.7 %collective-permute-start.11 = (bf16[448,1024]{1,0:T(8,128)(2,1)}, bf16[448,1024]{1,0:T(8,128)(2,1)S(1)}, u32[]{:S(2)}, u32[]{:S(2)}) collective-permute-start(bf16[448,1024]{1,0:T(8,128)(2,1)} %c0.15), channel_id=1, source_target_pairs={{0,1},{1,0},{2,3},{3,2},{4,5},{5,4},{6,7},{7,6},{8,9},{9,8},{10,11... | collective-permute-start | bytes 2752520 | tf_op jit(solution)/shard_map/ppermute | solution.py:149
  5.6 1.2 copy-start.4
  6.9 24.4 %collective-permute-start.6 = (bf16[256,1024]{1,0:T(8,128)(2,1)S(1)}, bf16[256,1024]{1,0:T(8,128)(2,1)S(1)}, u32[]{:S(2)}, u32[]{:S(2)}) collective-permute-start(bf16[256,1024]{1,0:T(8,128)(2,1)S(1)} %shard_map.90.refs_4_.wo), channel_id=1, source_target_pairs={{0,4},{1,5},{2,6},{3,7},{4,8},{5,9},{6,10},{7,11},{8,12},{9,13},{1... | collective-permute-start | bytes 1572872 | tf_op jit(solution)/shard_map/ppermute | solution.py:146
  20.9 12.2 %collective-permute-start.3 = (bf16[1024,256]{1,0:T(8,128)(2,1)S(1)}, bf16[1024,256]{1,0:T(8,128)(2,1)S(1)}, u32[]{:S(2)}, u32[]{:S(2)}) collective-permute-start(bf16[1024,256]{1,0:T(8,128)(2,1)S(1)} %collective-permute-done.2.wi.refs_6_), channel_id=1, source_target_pairs={{0,2},{1,3},{2,0},{3,1},{4,6},{5,7},{6,4},{7,5},{8,10},{9,11},{10,... | collective-permute-start | bytes 1572872 | tf_op jit(solution)/shard_map/ppermute | solution.py:146
  22.6 18.5 %collective-permute-start = (bf16[448,1024]{1,0:T(8,128)(2,1)S(1)}, bf16[448,1024]{1,0:T(8,128)(2,1)S(1)}, u32[]{:S(2)}, u32[]{:S(2)}) collective-permute-start(bf16[448,1024]{1,0:T(8,128)(2,1)S(1)} %copy-done.2), channel_id=1, source_target_pairs={{0,1},{1,0},{2,3},{3,2},{4,5},{5,4},{6,7},{7,6},{8,9},{9,8},{10,11... | collective-permute-start | bytes 2752520 | tf_op jit(solution)/shard_map/ppermute | solution.py:149
  31.3 37.3 %collective-permute-start.7 = (bf16[256,1024]{1,0:T(8,128)(2,1)S(1)}, bf16[256,1024]{1,0:T(8,128)(2,1)S(1)}, u32[]{:S(2)}, u32[]{:S(2)}) collective-permute-start(bf16[256,1024]{1,0:T(8,128)(2,1)S(1)} %collective-permute-done.6.refs_6_.wo), channel_id=1, source_target_pairs={{0,2},{1,3},{2,0},{3,1},{4,6},{5,7},{6,4},{7,5},{8,10},{9,11},{10,... | collective-permute-start | bytes 1572872 | tf_op jit(solution)/shard_map/ppermute | solution.py:146
  34.9 45.0 %collective-permute-start.18 = (bf16[256,1024]{1,0:T(8,128)(2,1)S(1)}, bf16[256,1024]{1,0:T(8,128)(2,1)S(1)}, u32[]{:S(2)}, u32[]{:S(2)}) collective-permute-start(bf16[256,1024]{1,0:T(8,128)(2,1)S(1)} %get-tuple-element.49), channel_id=1, source_target_pairs={{2,0},{3,1},{0,2},{1,3},{6,4},{7,5},{4,6},{5,7},{10,8},{11,9},{8,1... | collective-permute-start | bytes 1572872 | tf_op jit(solution)/shard_map/ppermute | solution.py:146
  36.3 52.7 %collective-permute-start.1 = (bf16[1024,256]{1,0:T(8,128)(2,1)S(1)}, bf16[1024,256]{1,0:T(8,128)(2,1)S(1)}, u32[]{:S(2)}, u32[]{:S(2)}) collective-permute-start(bf16[1024,256]{1,0:T(8,128)(2,1)S(1)} %shard_map.84.wi.refs_4_), channel_id=1, source_target_pairs={{0,2},{1,3},{2,8},{3,9},{4,6},{5,7},{8,10},{9,11},{10,16},{11,17},... | collective-permute-start | bytes 1572872 | tf_op jit(solution)/shard_map/ppermute | solution.py:146
  38.9 55.6 %collective-permute-start.5 = (bf16[256,1024]{1,0:T(8,128)(2,1)S(1)}, bf16[256,1024]{1,0:T(8,128)(2,1)S(1)}, u32[]{:S(2)}, u32[]{:S(2)}) collective-permute-start(bf16[256,1024]{1,0:T(8,128)(2,1)S(1)} %shard_map.90.refs_4_.wo), channel_id=1, source_target_pairs={{0,2},{1,3},{2,8},{3,9},{4,6},{5,7},{8,10},{9,11},{10,16},{11,17},... | collective-permute-start | bytes 1572872 | tf_op jit(solution)/shard_map/ppermute | solution.py:146
  41.9 47.3 %collective-permute-start.4 = (bf16[1024,256]{1,0:T(8,128)(2,1)S(1)}, bf16[1024,256]{1,0:T(8,128)(2,1)S(1)}, u32[]{:S(2)}, u32[]{:S(2)}) collective-permute-start(bf16[1024,256]{1,0:T(8,128)(2,1)S(1)} %collective-permute-done.3.wi.refs_7_), channel_id=1, source_target_pairs={{0,4},{1,5},{8,12},{9,13},{16,20},{17,21},{24,28},{25,29}} | collective-permute-start | bytes 1572872 | tf_op jit(solution)/shard_map/ppermute | solution.py:146
  69.9 21.2 %collective-permute-start.14 = (bf16[256,1024]{1,0:T(8,128)(2,1)S(1)}, bf16[256,1024]{1,0:T(8,128)(2,1)S(1)}, u32[]{:S(2)}, u32[]{:S(2)}) collective-permute-start(bf16[256,1024]{1,0:T(8,128)(2,1)S(1)} %get-tuple-element.43), channel_id=1, source_target_pairs={{2,0},{3,1},{0,2},{1,3},{6,4},{7,5},{4,6},{5,7},{10,8},{11,9},{8,1... | collective-permute-start | bytes 1572872 | tf_op jit(solution)/shard_map/ppermute | solution.py:146
  79.8 20.7 %collective-permute-start.8 = (bf16[256,1024]{1,0:T(8,128)(2,1)S(1)}, bf16[256,1024]{1,0:T(8,128)(2,1)S(1)}, u32[]{:S(2)}, u32[]{:S(2)}) collective-permute-start(bf16[256,1024]{1,0:T(8,128)(2,1)S(1)} %collective-permute-done.7.refs_7_.wo), channel_id=1, source_target_pairs={{0,4},{1,5},{8,12},{9,13},{16,20},{17,21},{24,28},{25,29}} | collective-permute-start | bytes 1572872 | tf_op jit(solution)/shard_map/ppermute | solution.py:146
  89.0 18.1 %collective-permute-start.19 = (bf16[256,1024]{1,0:T(8,128)(2,1)S(1)}, bf16[256,1024]{1,0:T(8,128)(2,1)S(1)}, u32[]{:S(2)}, u32[]{:S(2)}) collective-permute-start(bf16[256,1024]{1,0:T(8,128)(2,1)S(1)} %shard_map.107), channel_id=1, source_target_pairs={{4,0},{5,1},{6,2},{7,3},{8,4},{9,5},{10,6},{11,7},{12,8},{13,9},{1... | collective-permute-start | bytes 1572872 | tf_op jit(solution)/shard_map/ppermute | solution.py:146
  91.1 21.7 %collective-permute-start.17 = (bf16[256,1024]{1,0:T(8,128)(2,1)S(1)}, bf16[256,1024]{1,0:T(8,128)(2,1)S(1)}, u32[]{:S(2)}, u32[]{:S(2)}) collective-permute-start(bf16[256,1024]{1,0:T(8,128)(2,1)S(1)} %get-tuple-element.47), channel_id=1, source_target_pairs={{2,0},{3,1},{8,2},{9,3},{6,4},{7,5},{12,6},{13,7},{10,8},{11,9},{1... | collective-permute-start | bytes 1572872 | tf_op jit(solution)/shard_map/ppermute | solution.py:146
  91.3 32.7 %collective-permute-start.15 = (bf16[256,1024]{1,0:T(8,128)(2,1)S(1)}, bf16[256,1024]{1,0:T(8,128)(2,1)S(1)}, u32[]{:S(2)}, u32[]{:S(2)}) collective-permute-start(bf16[256,1024]{1,0:T(8,128)(2,1)S(1)} %shard_map.104), channel_id=1, source_target_pairs={{4,0},{5,1},{6,2},{7,3},{8,4},{9,5},{10,6},{11,7},{12,8},{13,9},{1... | collective-permute-start | bytes 1572872 | tf_op jit(solution)/shard_map/ppermute | solution.py:146
  102.0 29.3 %collective-permute-start.13 = (bf16[256,1024]{1,0:T(8,128)(2,1)S(1)}, bf16[256,1024]{1,0:T(8,128)(2,1)S(1)}, u32[]{:S(2)}, u32[]{:S(2)}) collective-permute-start(bf16[256,1024]{1,0:T(8,128)(2,1)S(1)} %get-tuple-element.41), channel_id=1, source_target_pairs={{2,0},{3,1},{8,2},{9,3},{6,4},{7,5},{12,6},{13,7},{10,8},{11,9},{1... | collective-permute-start | bytes 1572872 | tf_op jit(solution)/shard_map/ppermute | solution.py:146
  104.1 27.3 %collective-permute-start.12 = (bf16[448,1024]{1,0:T(8,128)(2,1)S(1)}, bf16[448,1024]{1,0:T(8,128)(2,1)S(1)}, u32[]{:S(2)}, u32[]{:S(2)}) collective-permute-start(bf16[448,1024]{1,0:T(8,128)(2,1)S(1)} %get-tuple-element.39), channel_id=1, source_target_pairs={{0,1},{1,0},{2,3},{3,2},{4,5},{5,4},{6,7},{7,6},{8,9},{9,8},{10,11... | collective-permute-start | bytes 2752520 | tf_op jit(solution)/shard_map/ppermute | solution.py:149
  107.1 25.5 %collective-permute-start.9 = (bf16[448,1024]{1,0:T(8,128)(2,1)S(1)}, bf16[448,1024]{1,0:T(8,128)(2,1)S(1)}, u32[]{:S(2)}, u32[]{:S(2)}) collective-permute-start(bf16[448,1024]{1,0:T(8,128)(2,1)S(1)} %get-tuple-element.29), channel_id=1, source_target_pairs={{0,1},{1,0},{2,3},{3,2},{4,5},{5,4},{6,7},{7,6},{8,9},{9,8},{10,11... | collective-permute-start | bytes 2752520 | tf_op jit(solution)/shard_map/ppermute | solution.py:149
  112.9 20.7 %collective-permute-start.20 = (f32[256,512]{1,0:T(8,128)S(1)}, f32[256,512]{1,0:T(8,128)S(1)}, u32[]{:S(2)}, u32[]{:S(2)}) collective-permute-start(f32[256,512]{1,0:T(8,128)S(1)} %get-tuple-element.51), channel_id=1, source_target_pairs={{0,1},{1,0},{2,3},{3,2},{4,5},{5,4},{6,7},{7,6},{8,9},{9,8},{10,11... | collective-permute-start | bytes 1572872 | tf_op jit(solution)/shard_map/ppermute | solution.py:149
  131.4 3.3 %collective-permute-start.16 = (f32[256,512]{1,0:T(8,128)S(1)}, f32[256,512]{1,0:T(8,128)S(1)}, u32[]{:S(2)}, u32[]{:S(2)}) collective-permute-start(f32[256,512]{1,0:T(8,128)S(1)} %get-tuple-element.45), channel_id=1, source_target_pairs={{0,1},{1,0},{2,3},{3,2},{4,5},{5,4},{6,7},{7,6},{8,9},{9,8},{10,11... | collective-permute-start | bytes 1572872 | tf_op jit(solution)/shard_map/ppermute | solution.py:149
where the time goes:
time: 136 us
  waiting for transfers between devices  86.1 us (63%)
  Pallas kernels  24.9 us (18%)
  starting transfers between devices  21.5 us (16%)
  local copies, waits for them, and re-layouts  2.59 us (2%)
    ppermute x14, waiting for transfers between devices, move(): return lax.ppermute(value, axes, pairs)  86.1 us
    pallas_call x26, Pallas kernels, call(): pl.pallas_call(body, out_shape=outs, in_specs=[pl.BlockSpec(memory_space=...  24.9 us
    ppermute x14, starting transfers between devices, move(): return lax.ppermute(value, axes, pairs)  20.2 us
  transfers between devices with their start and end apart: 21, of which 9 were waited for; matrix products, arithmetic and copies ran while one was open for 0% of the time, Pallas kernels for 17%

commit v1 on v0

--- a/solution.py
+++ b/solution.py
@@ -15,26 +15,37 @@
 F32, BF16 = jnp.float32, jnp.bfloat16
 
 
+WEIGHT_KINDS = {"i": "A", "o": "A"}
+GRAD_KINDS = {"d": "B", "n": "B"}
+
+
 def routes(n_blk, n_rep):
     groups = n_blk // TICKS
-    across, beside, returned, forward, third = [], [], [], [], []
+    names = ("across", "across_but", "beside", "beside_but_last", "side", "third", "turn", "over")
+    pairs = {name: [] for name in names}
     for blk in range(n_blk):
         group, place = blk // TICKS, blk % TICKS
         for rep in range(n_rep):
             source = blk * n_rep + rep
 
-            def target(to):
-                to_group = group + (1 if to < place else 0)
-                return ((to_group % groups) * TICKS + to) * n_rep + rep
-
-            returned.append((target(place ^ 1), source))
+            def at(to, later=0):
+                return (((group + later) % groups) * TICKS + to) * n_rep + rep
+
+            def add(name, to, later=0):
+                pairs[name].append((source, at(to, later)))
+
+            add("across", place ^ SIDE, place ^ SIDE < place)
+            add("beside", place ^ 1, place ^ 1 < place)
             if place < TICKS - 1:
-                beside.append((source, target(place ^ 1)))
+                add("beside_but_last", place ^ 1, place ^ 1 < place)
+            add("side", place ^ 1)
             if place == 0:
-                third.append((source, (group * TICKS + SIDE) * n_rep + rep))
-            across.append((source, target(place ^ SIDE)))
-            forward.append((source, (group * TICKS + (place ^ 1)) * n_rep + rep))
-    return beside, returned, across, forward, third
+                add("third", SIDE)
+                add("over", 1)
+            if place != SIDE:
+                add("across_but", place ^ SIDE, place ^ SIDE < place)
+            add("turn", place ^ SIDE, (place == TICKS - 1) - (place == 0))
+    return pairs
 
 
 def back(pairs):
@@ -135,7 +146,7 @@
 def window(fwd_in, bwd_in, cotangent, w_in, w_out):
     axes = ("blk", "rep")
     n_blk, n_rep = lax.axis_size("blk"), lax.axis_size("rep")
-    beside, returned, across, forward, third = routes(n_blk, n_rep)
+    pairs = routes(n_blk, n_rep)
     width = w_in.shape[1] // n_rep
     rows, model = fwd_in.shape
     span = model // n_rep
@@ -184,13 +195,19 @@
     def add(a, b):
         return run(add_kernel, shape(a.shape, BF16), unit // 4, a, b)
 
+    def spread(label, weight):
+        x = move(weight, pairs["beside"])
+        y = move(weight, pairs["across"])
+        if WEIGHT_KINDS[label] == "A":
+            d = move(y, pairs["side"])
+        else:
+            d = move(x, pairs["turn"])
+        return x, y, d
+
     wi, wo = cut(w_in, 1), cut(w_out, 0)
-    yi, xi = move(wi, across), move(wi, beside)
-    yo, xo = move(wo, across), move(wo, beside)
+    xi, yi, di = spread("i", wi)
+    xo, yo, do = spread("o", wo)
     bwd_peer, cot_peer, fwd_peer = peer(bwd_in), peer(cotangent), peer(fwd_in)
-    di, do = move(yi, forward), move(yo, forward)
-    xi = add(xi, move(di, third))
-    xo = add(xo, move(do, third))
 
     down_0, slope_0 = in_part(wi, F32)
     into_0, pre_0 = out_part(wo, slope_0, F32)
@@ -205,10 +222,19 @@
     into_x, pre_x = out_part(xo, slope_x, BF16)
     hid_x = fwd_part(xi)
 
-    down_y = add(down_y, move(down_d, back(forward)))
-    into_y = add(into_y, move(into_d, back(forward)))
-    down_across, into_across = move(down_y, back(across)), move(into_y, back(across))
-    down_beside, into_beside = move(down_x, returned), move(into_x, returned)
+    def gather(label, g_x, g_y, g_d):
+        rest = back(pairs["across"])
+        if GRAD_KINDS[label] == "C":
+            g_d = add(g_d, move(g_y, pairs["over"]))
+            rest = back(pairs["across_but"])
+        if GRAD_KINDS[label] == "A":
+            g_y = add(g_y, move(g_d, back(pairs["side"])))
+        else:
+            g_x = add(g_x, move(g_d, back(pairs["turn"])))
+        return (move(g_x, back(pairs["beside"])), move(g_y, rest))
+
+    down_beside, down_across = gather("d", down_x, down_y, down_d)
+    into_beside, into_across = gather("n", into_x, into_y, into_d)
 
     def sums(lefts, rights, dim):
         give, keep = run(

time: 136 us -> 119 us (0.88)
  waiting for transfers between devices: 86.1 us -> 56.2 us
  starting transfers between devices: 21.5 us -> 34.3 us
    ppermute x14 -> x12, waiting for transfers between devices: 86.1 us -> 56.2 us  [move(): return lax.ppermute(value, axes, pairs)]
    ppermute x14 -> x12, starting transfers between devices: 20.2 us -> 33 us  [move(): return lax.ppermute(value, axes, pairs)]
    pallas_call x26 -> x24, Pallas kernels: 24.9 us -> 24.6 us  [call(): pl.pallas_call(body, out_shape=outs, in_specs=[pl.BlockSpec(memory_space=...]
  transfers between devices with their start and end apart: 21 -> 19, of which waited for: 9 -> 7; matrix products, arithmetic and copies ran while one was open for 0% -> 0% of each run, Pallas kernels for 17% -> 20%
where the time goes in v1:
time: 119 us
  waiting for transfers between devices  56.2 us (47%)
  starting transfers between devices  34.3 us (29%)
  Pallas kernels  24.6 us (21%)
  local copies, waits for them, and re-layouts  2.46 us (2%)
    ppermute x12, waiting for transfers between devices, move(): return lax.ppermute(value, axes, pairs)  56.2 us
    ppermute x12, starting transfers between devices, move(): return lax.ppermute(value, axes, pairs)  33 us
    pallas_call x24, Pallas kernels, call(): pl.pallas_call(body, out_shape=outs, in_specs=[pl.BlockSpec(memory_space=...  24.6 us
    unnamed x10, local copies, waits for them, and re-layouts  2.46 us
  transfers between devices with their start and end apart: 19, of which 7 were waited for; matrix products, arithmetic and copies ran while one was open for 0% of the time, Pallas kernels for 20%

profile of v1, /device:TPU:0, one launch (start us, length us, event | category | flops | bytes accessed | tf_op | source)
XLA Modules:
  0.0 118.5 jit_solution(12072955171379852561)
XLA Ops:
  0.7 0.6 collective-permute-start.8
  1.2 0.1 collective-permute-start.9
  1.3 0.4 collective-permute-start
  1.7 1.2 %copy-done.3 = bf16[1024,512]{1,0:T(8,128)(2,1)S(1)} copy-done((bf16[1024,512]{1,0:T(8,128)(2,1)S(1)}, bf16[1024,512]{1,0:T(8,128)(2,1)}, u32[]{:S(2)}) %copy-start.3) | copy-done | bytes 1048600
  3.0 2.6 %collective-permute-start.2 = (bf16[1024,256]{1,0:T(8,128)(2,1)S(1)}, bf16[1024,256]{1,0:T(8,128)(2,1)S(1)}, u32[]{:S(2)}, u32[]{:S(2)}) collective-permute-start(bf16[1024,256]{1,0:T(8,128)(2,1)S(1)} %shard_map.84.wi.refs_4_), channel_id=1, source_target_pairs={{0,4},{1,5},{2,6},{3,7},{4,8},{5,9},{6,10},{7,11},{8,12},{9,13},{1... | collective-permute-start | bytes 1572872 | tf_op jit(solution)/shard_map/ppermute | solution.py:157
  5.6 1.2 %copy-done.4 = bf16[512,1024]{1,0:T(8,128)(2,1)S(1)} copy-done((bf16[512,1024]{1,0:T(8,128)(2,1)S(1)}, bf16[512,1024]{1,0:T(8,128)(2,1)}, u32[]{:S(2)}) %copy-start.4) | copy-done | bytes 1048600
  6.9 1.6 %collective-permute-start.5 = (bf16[256,1024]{1,0:T(8,128)(2,1)S(1)}, bf16[256,1024]{1,0:T(8,128)(2,1)S(1)}, u32[]{:S(2)}, u32[]{:S(2)}) collective-permute-start(bf16[256,1024]{1,0:T(8,128)(2,1)S(1)} %shard_map.89.refs_4_.wo), channel_id=1, source_target_pairs={{0,4},{1,5},{2,6},{3,7},{4,8},{5,9},{6,10},{7,11},{8,12},{9,13},{1... | collective-permute-start | bytes 1572872 | tf_op jit(solution)/shard_map/ppermute | solution.py:157
  8.5 13.0 %collective-permute-done.2.wi.refs_6_ = bf16[1024,256]{1,0:T(8,128)(2,1)S(1)} collective-permute-done((bf16[1024,256]{1,0:T(8,128)(2,1)S(1)}, bf16[1024,256]{1,0:T(8,128)(2,1)S(1)}, u32[]{:S(2)}, u32[]{:S(2)}) %collective-permute-start.2) | collective-permute-done | bytes 524320 | tf_op jit(solution)/shard_map/ppermute | solution.py:157
  21.4 1.6 %collective-permute-start.1 = (bf16[1024,256]{1,0:T(8,128)(2,1)S(1)}, bf16[1024,256]{1,0:T(8,128)(2,1)S(1)}, u32[]{:S(2)}, u32[]{:S(2)}) collective-permute-start(bf16[1024,256]{1,0:T(8,128)(2,1)S(1)} %shard_map.84.wi.refs_4_), channel_id=1, source_target_pairs={{0,2},{1,3},{2,8},{3,9},{4,6},{5,7},{6,12},{7,13},{8,10},{9,11},{1... | collective-permute-start | bytes 1572872 | tf_op jit(solution)/shard_map/ppermute | solution.py:157
  23.1 9.3 %collective-permute-done.5.refs_6_.wo = bf16[256,1024]{1,0:T(8,128)(2,1)S(1)} collective-permute-done((bf16[256,1024]{1,0:T(8,128)(2,1)S(1)}, bf16[256,1024]{1,0:T(8,128)(2,1)S(1)}, u32[]{:S(2)}, u32[]{:S(2)}) %collective-permute-start.5) | collective-permute-done | bytes 524320 | tf_op jit(solution)/shard_map/ppermute | solution.py:157
  32.4 1.9 %collective-permute-start.3 = (bf16[1024,256]{1,0:T(8,128)(2,1)S(1)}, bf16[1024,256]{1,0:T(8,128)(2,1)S(1)}, u32[]{:S(2)}, u32[]{:S(2)}) collective-permute-start(bf16[1024,256]{1,0:T(8,128)(2,1)S(1)} %collective-permute-done.2.wi.refs_6_), channel_id=1, source_target_pairs={{0,2},{1,3},{2,0},{3,1},{4,6},{5,7},{6,4},{7,5},{8,10},{9,11},{10,... | collective-permute-start | bytes 1572872 | tf_op jit(solution)/shard_map/ppermute | solution.py:157
  34.3 0.1 collective-permute-start.6
  34.5 1.9 %collective-permute-start.4 = (bf16[256,1024]{1,0:T(8,128)(2,1)S(1)}, bf16[256,1024]{1,0:T(8,128)(2,1)S(1)}, u32[]{:S(2)}, u32[]{:S(2)}) collective-permute-start(bf16[256,1024]{1,0:T(8,128)(2,1)S(1)} %shard_map.89.refs_4_.wo), channel_id=1, source_target_pairs={{0,2},{1,3},{2,8},{3,9},{4,6},{5,7},{6,12},{7,13},{8,10},{9,11},{1... | collective-permute-start | bytes 1572872 | tf_op jit(solution)/shard_map/ppermute | solution.py:157
  36.4 1.7 %shard_map.96 = (bf16[256,1024]{1,0:T(8,128)(2,1)S(1)}, f32[2,448,256]{2,1,0:T(8,128)S(1)}) custom-call(bf16[448,1024]{1,0:T(8,128)(2,1)S(1)} %copy-done, bf16[448,1024]{1,0:T(8,128)(2,1)S(1)} %collective-permute-done.8.b1, bf16[448,1024]{1,0:T(8,128)(2,1)S(1)} %copy-done.1, bf16[448,1024]{1,0:T(8,128)(2,1)S(1)} %collective-permute-done.9.c1, ...), custom_call_target="tpu_custom_call" | custom-call | flops 939524096 | bytes 4194304 | tf_op jit(solution)/shard_map/pallas_call | solution.py:135
  38.1 1.4 %collective-permute-start.17 = (bf16[256,1024]{1,0:T(8,128)(2,1)S(1)}, bf16[256,1024]{1,0:T(8,128)(2,1)S(1)}, u32[]{:S(2)}, u32[]{:S(2)}) collective-permute-start(bf16[256,1024]{1,0:T(8,128)(2,1)S(1)} %get-tuple-element.49), channel_id=1, source_target_pairs={{4,0},{5,1},{6,2},{7,3},{8,4},{9,5},{10,6},{11,7},{12,8},{13,9},{1... | collective-permute-start | bytes 1572872 | tf_op jit(solution)/shard_map/ppermute | solution.py:157
  39.4 0.8 shard_map.87.refs_2_
  40.3 1.3 %shard_map.97 = (bf16[256,1024]{1,0:T(8,128)(2,1)S(1)}, bf16[2,448,256]{2,1,0:T(8,128)(2,1)S(1)}) custom-call(bf16[448,1024]{1,0:T(8,128)(2,1)S(1)} %copy-done, bf16[448,1024]{1,0:T(8,128)(2,1)S(1)} %collective-permute-done.8.b1, bf16[448,1024]{1,0:T(8,128)(2,1)S(1)} %copy-done.1, bf16[448,1024]{1,0:T(8,128)(2,1)S(1)} %collective-permute-done.9.c1, ...), custom_call_target="tpu_custom_call" | custom-call | flops 939524096 | bytes 5111808 | tf_op jit(solution)/shard_map/pallas_call | solution.py:135
  41.6 5.3 %collective-permute-start.13 = (bf16[256,1024]{1,0:T(8,128)(2,1)S(1)}, bf16[256,1024]{1,0:T(8,128)(2,1)S(1)}, u32[]{:S(2)}, u32[]{:S(2)}) collective-permute-start(bf16[256,1024]{1,0:T(8,128)(2,1)S(1)} %get-tuple-element.43), channel_id=1, source_target_pairs={{4,0},{5,1},{6,2},{7,3},{8,4},{9,5},{10,6},{11,7},{12,8},{13,9},{1... | collective-permute-start | bytes 1572872 | tf_op jit(solution)/shard_map/ppermute | solution.py:157
  46.9 0.8 shard_map.86.refs_1_
  47.7 1.7 %shard_map.94 = (bf16[256,1024]{1,0:T(8,128)(2,1)S(1)}, f32[2,448,256]{2,1,0:T(8,128)S(1)}) custom-call(bf16[448,1024]{1,0:T(8,128)(2,1)S(1)} %copy-done, bf16[448,1024]{1,0:T(8,128)(2,1)S(1)} %collective-permute-done.8.b1, bf16[448,1024]{1,0:T(8,128)(2,1)S(1)} %copy-done.1, bf16[448,1024]{1,0:T(8,128)(2,1)S(1)} %collective-permute-done.9.c1, ...), custom_call_target="tpu_custom_call" | custom-call | flops 939524096 | bytes 4194304 | tf_op jit(solution)/shard_map/pallas_call | solution.py:135
  49.4 10.7 %collective-permute-done.3.wi.refs_7_ = bf16[1024,256]{1,0:T(8,128)(2,1)S(1)} collective-permute-done((bf16[1024,256]{1,0:T(8,128)(2,1)S(1)}, bf16[1024,256]{1,0:T(8,128)(2,1)S(1)}, u32[]{:S(2)}, u32[]{:S(2)}) %collective-permute-start.3) | collective-permute-done | bytes 524320 | tf_op jit(solution)/shard_map/ppermute | solution.py:157
  60.1 1.7 %shard_map.98 = (bf16[256,1024]{1,0:T(8,128)(2,1)S(1)}, f32[2,448,256]{2,1,0:T(8,128)S(1)}) custom-call(bf16[448,1024]{1,0:T(8,128)(2,1)S(1)} %copy-done, bf16[448,1024]{1,0:T(8,128)(2,1)S(1)} %collective-permute-done.8.b1, bf16[448,1024]{1,0:T(8,128)(2,1)S(1)} %copy-done.1, bf16[448,1024]{1,0:T(8,128)(2,1)S(1)} %collective-permute-done.9.c1, ...), custom_call_target="tpu_custom_call" | custom-call | flops 939524096 | bytes 4194304 | tf_op jit(solution)/shard_map/pallas_call | solution.py:135
  61.8 7.6 %collective-permute-start.15 = (bf16[256,1024]{1,0:T(8,128)(2,1)S(1)}, bf16[256,1024]{1,0:T(8,128)(2,1)S(1)}, u32[]{:S(2)}, u32[]{:S(2)}) collective-permute-start(bf16[256,1024]{1,0:T(8,128)(2,1)S(1)} %get-tuple-element.48), channel_id=1, source_target_pairs={{28,0},{29,1},{6,2},{7,3},{0,4},{1,5},{10,6},{11,7},{4,8},{5,9},{1... | collective-permute-start | bytes 1572872 | tf_op jit(solution)/shard_map/ppermute | solution.py:157
  69.5 1.8 %collective-permute-done.6.refs_7_.wo = bf16[256,1024]{1,0:T(8,128)(2,1)S(1)} collective-permute-done((bf16[256,1024]{1,0:T(8,128)(2,1)S(1)}, bf16[256,1024]{1,0:T(8,128)(2,1)S(1)}, u32[]{:S(2)}, u32[]{:S(2)}) %collective-permute-start.6) | collective-permute-done | bytes 524320 | tf_op jit(solution)/shard_map/ppermute | solution.py:157
  71.3 1.3 %shard_map.99 = (bf16[256,1024]{1,0:T(8,128)(2,1)S(1)}, bf16[2,448,256]{2,1,0:T(8,128)(2,1)S(1)}) custom-call(bf16[448,1024]{1,0:T(8,128)(2,1)S(1)} %copy-done, bf16[448,1024]{1,0:T(8,128)(2,1)S(1)} %collective-permute-done.8.b1, bf16[448,1024]{1,0:T(8,128)(2,1)S(1)} %copy-done.1, bf16[448,1024]{1,0:T(8,128)(2,1)S(1)} %collective-permute-done.9.c1, ...), custom_call_target="tpu_custom_call" | custom-call | flops 939524096 | bytes 5111808 | tf_op jit(solution)/shard_map/pallas_call | solution.py:135
  72.6 7.2 %collective-permute-start.11 = (bf16[256,1024]{1,0:T(8,128)(2,1)S(1)}, bf16[256,1024]{1,0:T(8,128)(2,1)S(1)}, u32[]{:S(2)}, u32[]{:S(2)}) collective-permute-start(bf16[256,1024]{1,0:T(8,128)(2,1)S(1)} %get-tuple-element.42), channel_id=1, source_target_pairs={{28,0},{29,1},{6,2},{7,3},{0,4},{1,5},{10,6},{11,7},{4,8},{5,9},{1... | collective-permute-start | bytes 1572872 | tf_op jit(solution)/shard_map/ppermute | solution.py:157
  79.8 1.7 %shard_map.92 = (f32[256,1024]{1,0:T(8,128)S(1)}, f32[2,448,256]{2,1,0:T(8,128)S(1)}) custom-call(bf16[448,1024]{1,0:T(8,128)(2,1)S(1)} %copy-done, bf16[448,1024]{1,0:T(8,128)(2,1)S(1)} %collective-permute-done.8.b1, bf16[448,1024]{1,0:T(8,128)(2,1)S(1)} %copy-done.1, bf16[448,1024]{1,0:T(8,128)(2,1)S(1)} %collective-permute-done.9.c1, ...), custom_call_target="tpu_custom_call" | custom-call | flops 939524096 | bytes 4194304 | tf_op jit(solution)/shard_map/pallas_call | solution.py:135
  81.5 1.3 %shard_map.93 = (f32[256,1024]{1,0:T(8,128)S(1)}, bf16[2,448,256]{2,1,0:T(8,128)(2,1)S(1)}) custom-call(bf16[448,1024]{1,0:T(8,128)(2,1)S(1)} %copy-done, bf16[448,1024]{1,0:T(8,128)(2,1)S(1)} %collective-permute-done.8.b1, bf16[448,1024]{1,0:T(8,128)(2,1)S(1)} %copy-done.1, bf16[448,1024]{1,0:T(8,128)(2,1)S(1)} %collective-permute-done.9.c1, ...), custom_call_target="tpu_custom_call" | custom-call | flops 939524096 | bytes 5111808 | tf_op jit(solution)/shard_map/pallas_call | solution.py:135
  82.8 0.8 shard_map.85.refs_0_
  83.7 1.3 %shard_map.95 = (bf16[256,1024]{1,0:T(8,128)(2,1)S(1)}, bf16[2,448,256]{2,1,0:T(8,128)(2,1)S(1)}) custom-call(bf16[448,1024]{1,0:T(8,128)(2,1)S(1)} %copy-done, bf16[448,1024]{1,0:T(8,128)(2,1)S(1)} %collective-permute-done.8.b1, bf16[448,1024]{1,0:T(8,128)(2,1)S(1)} %copy-done.1, bf16[448,1024]{1,0:T(8,128)(2,1)S(1)} %collective-permute-done.9.c1, ...), custom_call_target="tpu_custom_call" | custom-call | flops 939524096 | bytes 5111808 | tf_op jit(solution)/shard_map/pallas_call | solution.py:135
  85.0 2.1 %shard_map.100 = (bf16[448,1024]{1,0:T(8,128)(2,1)S(1)}, f32[448,1024]{1,0:T(8,128)S(1)}) custom-call(bf16[2,448,256]{2,1,0:T(8,128)(2,1)S(1)} %get-tuple-element.31.refs_0_, bf16[2,448,256]{2,1,0:T(8,128)(2,1)S(1)} %get-tuple-element.33.refs_1_, bf16[2,448,256]{2,1,0:T(8,128)(2,1)S(1)} %get-tuple-element.35.refs_2_, ...), custom_call_target="tpu_custom_call" | custom-call | flops 1879048192 | bytes 3932160 | tf_op jit(solution)/shard_map/pallas_call | solution.py:135
  87.2 0.8 shard_map.88.refs_3_
  88.0 0.1 shard_map.105
  88.1 1.2 %collective-permute-start.16 = (bf16[256,1024]{1,0:T(8,128)(2,1)S(1)}, bf16[256,1024]{1,0:T(8,128)(2,1)S(1)}, u32[]{:S(2)}, u32[]{:S(2)}) collective-permute-start(bf16[256,1024]{1,0:T(8,128)(2,1)S(1)} %shard_map.105), channel_id=1, source_target_pairs={{2,0},{3,1},{8,2},{9,3},{6,4},{7,5},{12,6},{13,7},{10,8},{11,9},{1... | collective-permute-start | bytes 1572872 | tf_op jit(solution)/shard_map/ppermute | solution.py:157
  89.4 5.0 %collective-permute-done.11.b = bf16[256,1024]{1,0:T(8,128)(2,1)S(1)} collective-permute-done((bf16[256,1024]{1,0:T(8,128)(2,1)S(1)}, bf16[256,1024]{1,0:T(8,128)(2,1)S(1)}, u32[]{:S(2)}, u32[]{:S(2)}) %collective-permute-start.11) | collective-permute-done | bytes 524320 | tf_op jit(solution)/shard_map/ppermute | solution.py:157
  94.4 0.1 shard_map.102
  94.5 0.5 collective-permute-start.12
  95.0 2.1 %shard_map.90 = (bf16[448,1024]{1,0:T(8,128)(2,1)S(1)}, f32[448,1024]{1,0:T(8,128)S(1)}) custom-call(bf16[2,448,256]{2,1,0:T(8,128)(2,1)S(1)} %shard_map.85.refs_0_, bf16[2,448,256]{2,1,0:T(8,128)(2,1)S(1)} %shard_map.86.refs_1_, bf16[2,448,256]{2,1,0:T(8,128)(2,1)S(1)} %shard_map.87.refs_2_, bf16[2,448,256]{2,1,0:T(8,128)(2,1)S(1)} %shard_map.88.refs_3_, ...), custom_call_target="tpu_custom_call" | custom-call | flops 1879048192 | bytes 3932160 | tf_op jit(solution)/shard_map/pallas_call | solution.py:135
  97.1 0.1 collective-permute-start.7
  97.1 5.9 %collective-permute-done.16.x = bf16[256,1024]{1,0:T(8,128)(2,1)S(1)} collective-permute-done((bf16[256,1024]{1,0:T(8,128)(2,1)S(1)}, bf16[256,1024]{1,0:T(8,128)(2,1)S(1)}, u32[]{:S(2)}, u32[]{:S(2)}) %collective-permute-start.16) | collective-permute-done | bytes 524320 | tf_op jit(solution)/shard_map/ppermute | solution.py:157
  103.0 0.2 shard_map.106
  103.2 10.5 %collective-permute-done.12.x = bf16[256,1024]{1,0:T(8,128)(2,1)S(1)} collective-permute-done((bf16[256,1024]{1,0:T(8,128)(2,1)S(1)}, bf16[256,1024]{1,0:T(8,128)(2,1)S(1)}, u32[]{:S(2)}, u32[]{:S(2)}) %collective-permute-start.12) | collective-permute-done | bytes 524320 | tf_op jit(solution)/shard_map/ppermute | solution.py:157
  113.8 0.2 shard_map.103
  113.9 0.1 collective-permute-start.14
  114.0 1.1 shard_map.101
  115.1 1.1 shard_map.91
  116.2 1.0 shard_map.107
  117.2 1.3 %shard_map.104 = f32[512,512]{1,0:T(8,128)} custom-call(f32[256,512]{1,0:T(8,128)S(1)} %get-tuple-element.44.keep, f32[256,512]{1,0:T(8,128)S(1)} %collective-permute-done.14.got), custom_call_target="tpu_custom_call" | custom-call | flops 117440512 | bytes 1048576 | tf_op jit(solution)/shard_map/pallas_call | solution.py:135
  (24 shorter events, 0.3 us)
Async XLA Ops:
  0.6 35.7 %copy-start = (bf16[448,1024]{1,0:T(8,128)(2,1)S(1)}, bf16[448,1024]{1,0:T(8,128)(2,1)}, u32[]{:S(2)}) copy-start(bf16[448,1024]{1,0:T(8,128)(2,1)} %b0.15) | copy-start | bytes 2752516
  0.6 35.7 %copy-start.1 = (bf16[448,1024]{1,0:T(8,128)(2,1)S(1)}, bf16[448,1024]{1,0:T(8,128)(2,1)}, u32[]{:S(2)}) copy-start(bf16[448,1024]{1,0:T(8,128)(2,1)} %c0.15) | copy-start | bytes 2752516
  0.7 33.7 %collective-permute-start.8 = (bf16[448,1024]{1,0:T(8,128)(2,1)}, bf16[448,1024]{1,0:T(8,128)(2,1)S(1)}, u32[]{:S(2)}, u32[]{:S(2)}) collective-permute-start(bf16[448,1024]{1,0:T(8,128)(2,1)} %b0.15), channel_id=1, source_target_pairs={{0,1},{1,0},{2,3},{3,2},{4,5},{5,4},{6,7},{7,6},{8,9},{9,8},{10,11... | collective-permute-start | bytes 2752520 | tf_op jit(solution)/shard_map/ppermute | solution.py:160
  1.2 33.3 %collective-permute-start.9 = (bf16[448,1024]{1,0:T(8,128)(2,1)}, bf16[448,1024]{1,0:T(8,128)(2,1)S(1)}, u32[]{:S(2)}, u32[]{:S(2)}) collective-permute-start(bf16[448,1024]{1,0:T(8,128)(2,1)} %c0.15), channel_id=1, source_target_pairs={{0,1},{1,0},{2,3},{3,2},{4,5},{5,4},{6,7},{7,6},{8,9},{9,8},{10,11... | collective-permute-start | bytes 2752520 | tf_op jit(solution)/shard_map/ppermute | solution.py:160
  1.3 36.8 %collective-permute-start = (bf16[448,1024]{1,0:T(8,128)(2,1)}, bf16[448,1024]{1,0:T(8,128)(2,1)S(1)}, u32[]{:S(2)}, u32[]{:S(2)}) collective-permute-start(bf16[448,1024]{1,0:T(8,128)(2,1)} %f0.7), channel_id=1, source_target_pairs={{0,1},{1,0},{2,3},{3,2},{4,5},{5,4},{6,7},{7,6},{8,9},{9,8},{10,11... | collective-permute-start | bytes 2752520 | tf_op jit(solution)/shard_map/ppermute | solution.py:160
  1.7 1.2 %copy-start.3 = (bf16[1024,512]{1,0:T(8,128)(2,1)S(1)}, bf16[1024,512]{1,0:T(8,128)(2,1)}, u32[]{:S(2)}) copy-start(bf16[1024,512]{1,0:T(8,128)(2,1)} %whole.2) | copy-start | bytes 3145732
  3.0 18.4 %collective-permute-start.2 = (bf16[1024,256]{1,0:T(8,128)(2,1)S(1)}, bf16[1024,256]{1,0:T(8,128)(2,1)S(1)}, u32[]{:S(2)}, u32[]{:S(2)}) collective-permute-start(bf16[1024,256]{1,0:T(8,128)(2,1)S(1)} %shard_map.84.wi.refs_4_), channel_id=1, source_target_pairs={{0,4},{1,5},{2,6},{3,7},{4,8},{5,9},{6,10},{7,11},{8,12},{9,13},{1... | collective-permute-start | bytes 1572872 | tf_op jit(solution)/shard_map/ppermute | solution.py:157
  5.6 1.2 %copy-start.4 = (bf16[512,1024]{1,0:T(8,128)(2,1)S(1)}, bf16[512,1024]{1,0:T(8,128)(2,1)}, u32[]{:S(2)}) copy-start(bf16[512,1024]{1,0:T(8,128)(2,1)} %whole.3) | copy-start | bytes 3145732
  6.9 32.5 %copy-start.2 = (bf16[448,1024]{1,0:T(8,128)(2,1)S(1)}, bf16[448,1024]{1,0:T(8,128)(2,1)}, u32[]{:S(2)}) copy-start(bf16[448,1024]{1,0:T(8,128)(2,1)} %f0.7) | copy-start | bytes 2752516
  6.9 25.5 %collective-permute-start.5 = (bf16[256,1024]{1,0:T(8,128)(2,1)S(1)}, bf16[256,1024]{1,0:T(8,128)(2,1)S(1)}, u32[]{:S(2)}, u32[]{:S(2)}) collective-permute-start(bf16[256,1024]{1,0:T(8,128)(2,1)S(1)} %shard_map.89.refs_4_.wo), channel_id=1, source_target_pairs={{0,4},{1,5},{2,6},{3,7},{4,8},{5,9},{6,10},{7,11},{8,12},{9,13},{1... | collective-permute-start | bytes 1572872 | tf_op jit(solution)/shard_map/ppermute | solution.py:157
  21.4 20.2 %collective-permute-start.1 = (bf16[1024,256]{1,0:T(8,128)(2,1)S(1)}, bf16[1024,256]{1,0:T(8,128)(2,1)S(1)}, u32[]{:S(2)}, u32[]{:S(2)}) collective-permute-start(bf16[1024,256]{1,0:T(8,128)(2,1)S(1)} %shard_map.84.wi.refs_4_), channel_id=1, source_target_pairs={{0,2},{1,3},{2,8},{3,9},{4,6},{5,7},{6,12},{7,13},{8,10},{9,11},{1... | collective-permute-start | bytes 1572872 | tf_op jit(solution)/shard_map/ppermute | solution.py:157
  32.4 27.7 %collective-permute-start.3 = (bf16[1024,256]{1,0:T(8,128)(2,1)S(1)}, bf16[1024,256]{1,0:T(8,128)(2,1)S(1)}, u32[]{:S(2)}, u32[]{:S(2)}) collective-permute-start(bf16[1024,256]{1,0:T(8,128)(2,1)S(1)} %collective-permute-done.2.wi.refs_6_), channel_id=1, source_target_pairs={{0,2},{1,3},{2,0},{3,1},{4,6},{5,7},{6,4},{7,5},{8,10},{9,11},{10,... | collective-permute-start | bytes 1572872 | tf_op jit(solution)/shard_map/ppermute | solution.py:157
  34.3 36.9 %collective-permute-start.6 = (bf16[256,1024]{1,0:T(8,128)(2,1)S(1)}, bf16[256,1024]{1,0:T(8,128)(2,1)S(1)}, u32[]{:S(2)}, u32[]{:S(2)}) collective-permute-start(bf16[256,1024]{1,0:T(8,128)(2,1)S(1)} %collective-permute-done.5.refs_6_.wo), channel_id=1, source_target_pairs={{0,2},{1,3},{2,0},{3,1},{4,6},{5,7},{6,4},{7,5},{8,10},{9,11},{10,... | collective-permute-start | bytes 1572872 | tf_op jit(solution)/shard_map/ppermute | solution.py:157
  34.5 49.2 %collective-permute-start.4 = (bf16[256,1024]{1,0:T(8,128)(2,1)S(1)}, bf16[256,1024]{1,0:T(8,128)(2,1)S(1)}, u32[]{:S(2)}, u32[]{:S(2)}) collective-permute-start(bf16[256,1024]{1,0:T(8,128)(2,1)S(1)} %shard_map.89.refs_4_.wo), channel_id=1, source_target_pairs={{0,2},{1,3},{2,8},{3,9},{4,6},{5,7},{6,12},{7,13},{8,10},{9,11},{1... | collective-permute-start | bytes 1572872 | tf_op jit(solution)/shard_map/ppermute | solution.py:157
  38.1 59.0 %collective-permute-start.17 = (bf16[256,1024]{1,0:T(8,128)(2,1)S(1)}, bf16[256,1024]{1,0:T(8,128)(2,1)S(1)}, u32[]{:S(2)}, u32[]{:S(2)}) collective-permute-start(bf16[256,1024]{1,0:T(8,128)(2,1)S(1)} %get-tuple-element.49), channel_id=1, source_target_pairs={{4,0},{5,1},{6,2},{7,3},{8,4},{9,5},{10,6},{11,7},{12,8},{13,9},{1... | collective-permute-start | bytes 1572872 | tf_op jit(solution)/shard_map/ppermute | solution.py:157
  41.6 61.6 %collective-permute-start.13 = (bf16[256,1024]{1,0:T(8,128)(2,1)S(1)}, bf16[256,1024]{1,0:T(8,128)(2,1)S(1)}, u32[]{:S(2)}, u32[]{:S(2)}) collective-permute-start(bf16[256,1024]{1,0:T(8,128)(2,1)S(1)} %get-tuple-element.43), channel_id=1, source_target_pairs={{4,0},{5,1},{6,2},{7,3},{8,4},{9,5},{10,6},{11,7},{12,8},{13,9},{1... | collective-permute-start | bytes 1572872 | tf_op jit(solution)/shard_map/ppermute | solution.py:157
  61.8 26.2 %collective-permute-start.15 = (bf16[256,1024]{1,0:T(8,128)(2,1)S(1)}, bf16[256,1024]{1,0:T(8,128)(2,1)S(1)}, u32[]{:S(2)}, u32[]{:S(2)}) collective-permute-start(bf16[256,1024]{1,0:T(8,128)(2,1)S(1)} %get-tuple-element.48), channel_id=1, source_target_pairs={{28,0},{29,1},{6,2},{7,3},{0,4},{1,5},{10,6},{11,7},{4,8},{5,9},{1... | collective-permute-start | bytes 1572872 | tf_op jit(solution)/shard_map/ppermute | solution.py:157
  72.6 21.8 %collective-permute-start.11 = (bf16[256,1024]{1,0:T(8,128)(2,1)S(1)}, bf16[256,1024]{1,0:T(8,128)(2,1)S(1)}, u32[]{:S(2)}, u32[]{:S(2)}) collective-permute-start(bf16[256,1024]{1,0:T(8,128)(2,1)S(1)} %get-tuple-element.42), channel_id=1, source_target_pairs={{28,0},{29,1},{6,2},{7,3},{0,4},{1,5},{10,6},{11,7},{4,8},{5,9},{1... | collective-permute-start | bytes 1572872 | tf_op jit(solution)/shard_map/ppermute | solution.py:157
  87.1 26.9 %collective-permute-start.10 = (bf16[448,1024]{1,0:T(8,128)(2,1)S(1)}, bf16[448,1024]{1,0:T(8,128)(2,1)S(1)}, u32[]{:S(2)}, u32[]{:S(2)}) collective-permute-start(bf16[448,1024]{1,0:T(8,128)(2,1)S(1)} %get-tuple-element.39), channel_id=1, source_target_pairs={{0,1},{1,0},{2,3},{3,2},{4,5},{5,4},{6,7},{7,6},{8,9},{9,8},{10,11... | collective-permute-start | bytes 2752520 | tf_op jit(solution)/shard_map/ppermute | solution.py:160
  88.1 14.8 %collective-permute-start.16 = (bf16[256,1024]{1,0:T(8,128)(2,1)S(1)}, bf16[256,1024]{1,0:T(8,128)(2,1)S(1)}, u32[]{:S(2)}, u32[]{:S(2)}) collective-permute-start(bf16[256,1024]{1,0:T(8,128)(2,1)S(1)} %shard_map.105), channel_id=1, source_target_pairs={{2,0},{3,1},{8,2},{9,3},{6,4},{7,5},{12,6},{13,7},{10,8},{11,9},{1... | collective-permute-start | bytes 1572872 | tf_op jit(solution)/shard_map/ppermute | solution.py:157
  94.5 19.2 %collective-permute-start.12 = (bf16[256,1024]{1,0:T(8,128)(2,1)S(1)}, bf16[256,1024]{1,0:T(8,128)(2,1)S(1)}, u32[]{:S(2)}, u32[]{:S(2)}) collective-permute-start(bf16[256,1024]{1,0:T(8,128)(2,1)S(1)} %shard_map.102), channel_id=1, source_target_pairs={{2,0},{3,1},{8,2},{9,3},{6,4},{7,5},{12,6},{13,7},{10,8},{11,9},{1... | collective-permute-start | bytes 1572872 | tf_op jit(solution)/shard_map/ppermute | solution.py:157
  97.1 18.0 %collective-permute-start.7 = (bf16[448,1024]{1,0:T(8,128)(2,1)S(1)}, bf16[448,1024]{1,0:T(8,128)(2,1)S(1)}, u32[]{:S(2)}, u32[]{:S(2)}) collective-permute-start(bf16[448,1024]{1,0:T(8,128)(2,1)S(1)} %get-tuple-element.29), channel_id=1, source_target_pairs={{0,1},{1,0},{2,3},{3,2},{4,5},{5,4},{6,7},{7,6},{8,9},{9,8},{10,11... | collective-permute-start | bytes 2752520 | tf_op jit(solution)/shard_map/ppermute | solution.py:160
  103.1 13.0 %collective-permute-start.18 = (f32[256,512]{1,0:T(8,128)S(1)}, f32[256,512]{1,0:T(8,128)S(1)}, u32[]{:S(2)}, u32[]{:S(2)}) collective-permute-start(f32[256,512]{1,0:T(8,128)S(1)} %get-tuple-element.51), channel_id=1, source_target_pairs={{0,1},{1,0},{2,3},{3,2},{4,5},{5,4},{6,7},{7,6},{8,9},{9,8},{10,11... | collective-permute-start | bytes 1572872 | tf_op jit(solution)/shard_map/ppermute | solution.py:160
  113.9 3.3 %collective-permute-start.14 = (f32[256,512]{1,0:T(8,128)S(1)}, f32[256,512]{1,0:T(8,128)S(1)}, u32[]{:S(2)}, u32[]{:S(2)}) collective-permute-start(f32[256,512]{1,0:T(8,128)S(1)} %get-tuple-element.45), channel_id=1, source_target_pairs={{0,1},{1,0},{2,3},{3,2},{4,5},{5,4},{6,7},{7,6},{8,9},{9,8},{10,11... | collective-permute-start | bytes 1572872 | tf_op jit(solution)/shard_map/ppermute | solution.py:160

commit v2 on v1

--- a/solution.py
+++ b/solution.py
@@ -116,7 +116,8 @@
     rep, size = lax.axis_index("rep"), keep.shape[1]
     for out, at in ((give, 1 - rep), (keep, rep)):
         where = pl.ds(pl.multiple_of(at * size, size), size)
-        out[...] = own[:, where] + x[:, where].astype(F32) + y[:, where].astype(F32)
+        total = own[:, where] + x[:, where].astype(F32) + y[:, where].astype(F32)
+        out[...] = total.astype(out.dtype)
 
 
 def join_kernel(dim, keep, got, out):
@@ -124,9 +125,9 @@
     for part, at in ((keep, rep), (got, 1 - rep)):
         where = pl.ds(pl.multiple_of(at * size, size), size)
         if dim:
-            out[:, where] = part[...].T
-        else:
-            out[where, :] = part[...]
+            out[:, where] = part[...].astype(F32).T
+        else:
+            out[where, :] = part[...].astype(F32)
 
 
 def call(body, outs, flops, *args, scratch=(), far=False):
@@ -253,7 +254,8 @@
 
     def share(own, x, y, dim):
         half = shape((width, span), F32)
-        keep, give = run(split_kernel, (half, half), unit // 4, own, x, y)
+        sent = shape((width, span), BF16)
+        keep, give = run(split_kernel, (half, sent), unit // 4, own, x, y)
         size = (span, n_rep * width) if dim else (n_rep * width, span)
         return run(
             functools.partial(join_kernel, dim), shape(size, F32), unit // 4,

time: 119 us -> 133 us (1.12)
  waiting for transfers between devices: 56.2 us -> 82.7 us
  starting transfers between devices: 34.3 us -> 22.4 us
    ppermute x12, waiting for transfers between devices: 56.2 us -> 82.7 us  [move(): return lax.ppermute(value, axes, pairs)]
    ppermute x12, starting transfers between devices: 33 us -> 21 us  [move(): return lax.ppermute(value, axes, pairs)]
  transfers between devices with their start and end apart: 19 -> 19, of which waited for: 7 -> 8; matrix products, arithmetic and copies ran while one was open for 0% -> 0% of each run, Pallas kernels for 20% -> 18%
where the time goes in v2:
time: 133 us
  waiting for transfers between devices  82.7 us (62%)
  Pallas kernels  24.6 us (18%)
  starting transfers between devices  22.4 us (17%)
  local copies, waits for them, and re-layouts  2.46 us (2%)
    ppermute x12, waiting for transfers between devices, move(): return lax.ppermute(value, axes, pairs)  82.7 us
    pallas_call x24, Pallas kernels, call(): pl.pallas_call(body, out_shape=outs, in_specs=[pl.BlockSpec(memory_space=...  24.6 us
    ppermute x12, starting transfers between devices, move(): return lax.ppermute(value, axes, pairs)  21 us
  transfers between devices with their start and end apart: 19, of which 8 were waited for; matrix products, arithmetic and copies ran while one was open for 0% of the time, Pallas kernels for 18%

profile of v2, /device:TPU:0, one launch (start us, length us, event | category | flops | bytes accessed | tf_op | source)
XLA Modules:
  0.0 133.0 jit_solution(6492691492221724128)
XLA Ops:
  0.7 0.6 collective-permute-start.8
  1.2 0.1 collective-permute-start.9
  1.3 1.2 copy-done.3
  2.6 3.0 %collective-permute-start.5 = (bf16[256,1024]{1,0:T(8,128)(2,1)S(1)}, bf16[256,1024]{1,0:T(8,128)(2,1)S(1)}, u32[]{:S(2)}, u32[]{:S(2)}) collective-permute-start(bf16[256,1024]{1,0:T(8,128)(2,1)S(1)} %shard_map.89.refs_4_.wo), channel_id=1, source_target_pairs={{0,4},{1,5},{2,6},{3,7},{4,8},{5,9},{6,10},{7,11},{8,12},{9,13},{1... | collective-permute-start | bytes 1572872 | tf_op jit(solution)/shard_map/ppermute | solution.py:158
  5.6 1.2 copy-done.4
  6.8 1.6 %collective-permute-start.2 = (bf16[1024,256]{1,0:T(8,128)(2,1)S(1)}, bf16[1024,256]{1,0:T(8,128)(2,1)S(1)}, u32[]{:S(2)}, u32[]{:S(2)}) collective-permute-start(bf16[1024,256]{1,0:T(8,128)(2,1)S(1)} %shard_map.84.wi.refs_4_), channel_id=1, source_target_pairs={{0,4},{1,5},{2,6},{3,7},{4,8},{5,9},{6,10},{7,11},{8,12},{9,13},{1... | collective-permute-start | bytes 1572872 | tf_op jit(solution)/shard_map/ppermute | solution.py:158
  8.4 12.9 %collective-permute-done.5.refs_6_.wo = bf16[256,1024]{1,0:T(8,128)(2,1)S(1)} collective-permute-done((bf16[256,1024]{1,0:T(8,128)(2,1)S(1)}, bf16[256,1024]{1,0:T(8,128)(2,1)S(1)}, u32[]{:S(2)}, u32[]{:S(2)}) %collective-permute-start.5) | collective-permute-done | bytes 524320 | tf_op jit(solution)/shard_map/ppermute | solution.py:158
  21.4 1.6 %collective-permute-start.1 = (bf16[1024,256]{1,0:T(8,128)(2,1)S(1)}, bf16[1024,256]{1,0:T(8,128)(2,1)S(1)}, u32[]{:S(2)}, u32[]{:S(2)}) collective-permute-start(bf16[1024,256]{1,0:T(8,128)(2,1)S(1)} %shard_map.84.wi.refs_4_), channel_id=1, source_target_pairs={{0,2},{1,3},{2,8},{3,9},{4,6},{5,7},{6,12},{7,13},{8,10},{9,11},{1... | collective-permute-start | bytes 1572872 | tf_op jit(solution)/shard_map/ppermute | solution.py:158
  23.0 9.0 %collective-permute-done.2.wi.refs_6_ = bf16[1024,256]{1,0:T(8,128)(2,1)S(1)} collective-permute-done((bf16[1024,256]{1,0:T(8,128)(2,1)S(1)}, bf16[1024,256]{1,0:T(8,128)(2,1)S(1)}, u32[]{:S(2)}, u32[]{:S(2)}) %collective-permute-start.2) | collective-permute-done | bytes 524320 | tf_op jit(solution)/shard_map/ppermute | solution.py:158
  32.0 2.3 %collective-permute-start.4 = (bf16[256,1024]{1,0:T(8,128)(2,1)S(1)}, bf16[256,1024]{1,0:T(8,128)(2,1)S(1)}, u32[]{:S(2)}, u32[]{:S(2)}) collective-permute-start(bf16[256,1024]{1,0:T(8,128)(2,1)S(1)} %shard_map.89.refs_4_.wo), channel_id=1, source_target_pairs={{0,2},{1,3},{2,8},{3,9},{4,6},{5,7},{6,12},{7,13},{8,10},{9,11},{1... | collective-permute-start | bytes 1572872 | tf_op jit(solution)/shard_map/ppermute | solution.py:158
  34.3 2.0 %collective-permute-start.3 = (bf16[1024,256]{1,0:T(8,128)(2,1)S(1)}, bf16[1024,256]{1,0:T(8,128)(2,1)S(1)}, u32[]{:S(2)}, u32[]{:S(2)}) collective-permute-start(bf16[1024,256]{1,0:T(8,128)(2,1)S(1)} %collective-permute-done.2.wi.refs_6_), channel_id=1, source_target_pairs={{0,2},{1,3},{2,0},{3,1},{4,6},{5,7},{6,4},{7,5},{8,10},{9,11},{10,... | collective-permute-start | bytes 1572872 | tf_op jit(solution)/shard_map/ppermute | solution.py:158
  36.3 1.7 %shard_map.96 = (bf16[256,1024]{1,0:T(8,128)(2,1)S(1)}, f32[2,448,256]{2,1,0:T(8,128)S(1)}) custom-call(bf16[448,1024]{1,0:T(8,128)(2,1)S(1)} %copy-done, bf16[448,1024]{1,0:T(8,128)(2,1)S(1)} %collective-permute-done.8.b1, bf16[448,1024]{1,0:T(8,128)(2,1)S(1)} %copy-done.1, bf16[448,1024]{1,0:T(8,128)(2,1)S(1)} %collective-permute-done.9.c1, ...), custom_call_target="tpu_custom_call" | custom-call | flops 939524096 | bytes 4194304 | tf_op jit(solution)/shard_map/pallas_call | solution.py:136
  38.0 1.0 collective-permute-start.17
  39.0 0.8 shard_map.87.refs_2_
  39.8 0.8 shard_map.85.refs_0_
  40.7 0.8 shard_map.86.refs_1_
  41.5 1.7 %shard_map.94 = (bf16[256,1024]{1,0:T(8,128)(2,1)S(1)}, f32[2,448,256]{2,1,0:T(8,128)S(1)}) custom-call(bf16[448,1024]{1,0:T(8,128)(2,1)S(1)} %copy-done, bf16[448,1024]{1,0:T(8,128)(2,1)S(1)} %collective-permute-done.8.b1, bf16[448,1024]{1,0:T(8,128)(2,1)S(1)} %copy-done.1, bf16[448,1024]{1,0:T(8,128)(2,1)S(1)} %collective-permute-done.9.c1, ...), custom_call_target="tpu_custom_call" | custom-call | flops 939524096 | bytes 4194304 | tf_op jit(solution)/shard_map/pallas_call | solution.py:136
  43.2 1.7 %shard_map.92 = (f32[256,1024]{1,0:T(8,128)S(1)}, f32[2,448,256]{2,1,0:T(8,128)S(1)}) custom-call(bf16[448,1024]{1,0:T(8,128)(2,1)S(1)} %copy-done, bf16[448,1024]{1,0:T(8,128)(2,1)S(1)} %collective-permute-done.8.b1, bf16[448,1024]{1,0:T(8,128)(2,1)S(1)} %copy-done.1, bf16[448,1024]{1,0:T(8,128)(2,1)S(1)} %collective-permute-done.9.c1, ...), custom_call_target="tpu_custom_call" | custom-call | flops 939524096 | bytes 4194304 | tf_op jit(solution)/shard_map/pallas_call | solution.py:136
  44.9 1.3 %shard_map.97 = (bf16[256,1024]{1,0:T(8,128)(2,1)S(1)}, bf16[2,448,256]{2,1,0:T(8,128)(2,1)S(1)}) custom-call(bf16[448,1024]{1,0:T(8,128)(2,1)S(1)} %copy-done, bf16[448,1024]{1,0:T(8,128)(2,1)S(1)} %collective-permute-done.8.b1, bf16[448,1024]{1,0:T(8,128)(2,1)S(1)} %copy-done.1, bf16[448,1024]{1,0:T(8,128)(2,1)S(1)} %collective-permute-done.9.c1, ...), custom_call_target="tpu_custom_call" | custom-call | flops 939524096 | bytes 5111808 | tf_op jit(solution)/shard_map/pallas_call | solution.py:136
  46.2 1.3 %shard_map.93 = (f32[256,1024]{1,0:T(8,128)S(1)}, bf16[2,448,256]{2,1,0:T(8,128)(2,1)S(1)}) custom-call(bf16[448,1024]{1,0:T(8,128)(2,1)S(1)} %copy-done, bf16[448,1024]{1,0:T(8,128)(2,1)S(1)} %collective-permute-done.8.b1, bf16[448,1024]{1,0:T(8,128)(2,1)S(1)} %copy-done.1, bf16[448,1024]{1,0:T(8,128)(2,1)S(1)} %collective-permute-done.9.c1, ...), custom_call_target="tpu_custom_call" | custom-call | flops 939524096 | bytes 5111808 | tf_op jit(solution)/shard_map/pallas_call | solution.py:136
  47.6 2.0 %collective-permute-done.4.refs_5_.wo = bf16[256,1024]{1,0:T(8,128)(2,1)S(1)} collective-permute-done((bf16[256,1024]{1,0:T(8,128)(2,1)S(1)}, bf16[256,1024]{1,0:T(8,128)(2,1)S(1)}, u32[]{:S(2)}, u32[]{:S(2)}) %collective-permute-start.4) | collective-permute-done | bytes 524320 | tf_op jit(solution)/shard_map/ppermute | solution.py:158
  49.5 1.3 %shard_map.95 = (bf16[256,1024]{1,0:T(8,128)(2,1)S(1)}, bf16[2,448,256]{2,1,0:T(8,128)(2,1)S(1)}) custom-call(bf16[448,1024]{1,0:T(8,128)(2,1)S(1)} %copy-done, bf16[448,1024]{1,0:T(8,128)(2,1)S(1)} %collective-permute-done.8.b1, bf16[448,1024]{1,0:T(8,128)(2,1)S(1)} %copy-done.1, bf16[448,1024]{1,0:T(8,128)(2,1)S(1)} %collective-permute-done.9.c1, ...), custom_call_target="tpu_custom_call" | custom-call | flops 939524096 | bytes 5111808 | tf_op jit(solution)/shard_map/pallas_call | solution.py:136
  50.9 19.6 %collective-permute-done.3.wi.refs_7_ = bf16[1024,256]{1,0:T(8,128)(2,1)S(1)} collective-permute-done((bf16[1024,256]{1,0:T(8,128)(2,1)S(1)}, bf16[1024,256]{1,0:T(8,128)(2,1)S(1)}, u32[]{:S(2)}, u32[]{:S(2)}) %collective-permute-start.3) | collective-permute-done | bytes 524320 | tf_op jit(solution)/shard_map/ppermute | solution.py:158
  70.5 1.7 %shard_map.98 = (bf16[256,1024]{1,0:T(8,128)(2,1)S(1)}, f32[2,448,256]{2,1,0:T(8,128)S(1)}) custom-call(bf16[448,1024]{1,0:T(8,128)(2,1)S(1)} %copy-done, bf16[448,1024]{1,0:T(8,128)(2,1)S(1)} %collective-permute-done.8.b1, bf16[448,1024]{1,0:T(8,128)(2,1)S(1)} %copy-done.1, bf16[448,1024]{1,0:T(8,128)(2,1)S(1)} %collective-permute-done.9.c1, ...), custom_call_target="tpu_custom_call" | custom-call | flops 939524096 | bytes 4194304 | tf_op jit(solution)/shard_map/pallas_call | solution.py:136
  72.2 7.9 %collective-permute-start.15 = (bf16[256,1024]{1,0:T(8,128)(2,1)S(1)}, bf16[256,1024]{1,0:T(8,128)(2,1)S(1)}, u32[]{:S(2)}, u32[]{:S(2)}) collective-permute-start(bf16[256,1024]{1,0:T(8,128)(2,1)S(1)} %get-tuple-element.48), channel_id=1, source_target_pairs={{28,0},{29,1},{6,2},{7,3},{0,4},{1,5},{10,6},{11,7},{4,8},{5,9},{1... | collective-permute-start | bytes 1572872 | tf_op jit(solution)/shard_map/ppermute | solution.py:158
  80.1 1.3 %shard_map.99 = (bf16[256,1024]{1,0:T(8,128)(2,1)S(1)}, bf16[2,448,256]{2,1,0:T(8,128)(2,1)S(1)}) custom-call(bf16[448,1024]{1,0:T(8,128)(2,1)S(1)} %copy-done, bf16[448,1024]{1,0:T(8,128)(2,1)S(1)} %collective-permute-done.8.b1, bf16[448,1024]{1,0:T(8,128)(2,1)S(1)} %copy-done.1, bf16[448,1024]{1,0:T(8,128)(2,1)S(1)} %collective-permute-done.9.c1, ...), custom_call_target="tpu_custom_call" | custom-call | flops 939524096 | bytes 5111808 | tf_op jit(solution)/shard_map/pallas_call | solution.py:136
  81.4 0.1 collective-permute-start.11
  81.5 0.8 shard_map.88.refs_3_
  82.3 2.1 %shard_map.90 = (bf16[448,1024]{1,0:T(8,128)(2,1)S(1)}, f32[448,1024]{1,0:T(8,128)S(1)}) custom-call(bf16[2,448,256]{2,1,0:T(8,128)(2,1)S(1)} %shard_map.85.refs_0_, bf16[2,448,256]{2,1,0:T(8,128)(2,1)S(1)} %shard_map.86.refs_1_, bf16[2,448,256]{2,1,0:T(8,128)(2,1)S(1)} %shard_map.87.refs_2_, bf16[2,448,256]{2,1,0:T(8,128)(2,1)S(1)} %shard_map.88.refs_3_, ...), custom_call_target="tpu_custom_call" | custom-call | flops 1879048192 | bytes 3932160 | tf_op jit(solution)/shard_map/pallas_call | solution.py:136
  84.4 0.1 collective-permute-start.7
  84.5 2.1 %shard_map.100 = (bf16[448,1024]{1,0:T(8,128)(2,1)S(1)}, f32[448,1024]{1,0:T(8,128)S(1)}) custom-call(bf16[2,448,256]{2,1,0:T(8,128)(2,1)S(1)} %get-tuple-element.31.refs_0_, bf16[2,448,256]{2,1,0:T(8,128)(2,1)S(1)} %get-tuple-element.33.refs_1_, bf16[2,448,256]{2,1,0:T(8,128)(2,1)S(1)} %get-tuple-element.35.refs_2_, ...), custom_call_target="tpu_custom_call" | custom-call | flops 1879048192 | bytes 3932160 | tf_op jit(solution)/shard_map/pallas_call | solution.py:136
  86.6 0.6 collective-permute-start.10
  87.1 7.1 %collective-permute-done.15.b = bf16[256,1024]{1,0:T(8,128)(2,1)S(1)} collective-permute-done((bf16[256,1024]{1,0:T(8,128)(2,1)S(1)}, bf16[256,1024]{1,0:T(8,128)(2,1)S(1)}, u32[]{:S(2)}, u32[]{:S(2)}) %collective-permute-start.15) | collective-permute-done | bytes 524320 | tf_op jit(solution)/shard_map/ppermute | solution.py:158
  94.2 0.1 shard_map.105
  94.4 11.1 %collective-permute-done.11.b = bf16[256,1024]{1,0:T(8,128)(2,1)S(1)} collective-permute-done((bf16[256,1024]{1,0:T(8,128)(2,1)S(1)}, bf16[256,1024]{1,0:T(8,128)(2,1)S(1)}, u32[]{:S(2)}, u32[]{:S(2)}) %collective-permute-start.11) | collective-permute-done | bytes 524320 | tf_op jit(solution)/shard_map/ppermute | solution.py:158
  105.5 1.0 collective-permute-start.13
  106.5 0.1 shard_map.102
  106.7 0.4 collective-permute-start.12
  107.1 0.2 shard_map.106
  107.2 0.1 collective-permute-start.18
  107.3 11.5 %collective-permute-done.13.y = bf16[256,1024]{1,0:T(8,128)(2,1)S(1)} collective-permute-done((bf16[256,1024]{1,0:T(8,128)(2,1)S(1)}, bf16[256,1024]{1,0:T(8,128)(2,1)S(1)}, u32[]{:S(2)}, u32[]{:S(2)}) %collective-permute-start.13) | collective-permute-done | bytes 524320 | tf_op jit(solution)/shard_map/ppermute | solution.py:158
  118.9 9.4 %collective-permute-done.12.x = bf16[256,1024]{1,0:T(8,128)(2,1)S(1)} collective-permute-done((bf16[256,1024]{1,0:T(8,128)(2,1)S(1)}, bf16[256,1024]{1,0:T(8,128)(2,1)S(1)}, u32[]{:S(2)}, u32[]{:S(2)}) %collective-permute-start.12) | collective-permute-done | bytes 524320 | tf_op jit(solution)/shard_map/ppermute | solution.py:158
  128.3 0.2 shard_map.103
  128.4 0.1 collective-permute-start.14
  128.5 1.1 shard_map.91
  129.6 1.1 shard_map.101
  130.7 1.0 shard_map.107
  131.7 1.3 shard_map.104
  (24 shorter events, 0.2 us)
Async XLA Ops:
  0.6 35.7 %copy-start = (bf16[448,1024]{1,0:T(8,128)(2,1)S(1)}, bf16[448,1024]{1,0:T(8,128)(2,1)}, u32[]{:S(2)}) copy-start(bf16[448,1024]{1,0:T(8,128)(2,1)} %b0.15) | copy-start | bytes 2752516
  0.6 35.7 %copy-start.1 = (bf16[448,1024]{1,0:T(8,128)(2,1)S(1)}, bf16[448,1024]{1,0:T(8,128)(2,1)}, u32[]{:S(2)}) copy-start(bf16[448,1024]{1,0:T(8,128)(2,1)} %c0.15) | copy-start | bytes 2752516
  0.7 33.6 %collective-permute-start.8 = (bf16[448,1024]{1,0:T(8,128)(2,1)}, bf16[448,1024]{1,0:T(8,128)(2,1)S(1)}, u32[]{:S(2)}, u32[]{:S(2)}) collective-permute-start(bf16[448,1024]{1,0:T(8,128)(2,1)} %b0.15), channel_id=1, source_target_pairs={{0,1},{1,0},{2,3},{3,2},{4,5},{5,4},{6,7},{7,6},{8,9},{9,8},{10,11... | collective-permute-start | bytes 2752520 | tf_op jit(solution)/shard_map/ppermute | solution.py:161
  1.2 33.1 %collective-permute-start.9 = (bf16[448,1024]{1,0:T(8,128)(2,1)}, bf16[448,1024]{1,0:T(8,128)(2,1)S(1)}, u32[]{:S(2)}, u32[]{:S(2)}) collective-permute-start(bf16[448,1024]{1,0:T(8,128)(2,1)} %c0.15), channel_id=1, source_target_pairs={{0,1},{1,0},{2,3},{3,2},{4,5},{5,4},{6,7},{7,6},{8,9},{9,8},{10,11... | collective-permute-start | bytes 2752520 | tf_op jit(solution)/shard_map/ppermute | solution.py:161
  1.3 1.2 copy-start.3
  2.6 18.8 %collective-permute-start.5 = (bf16[256,1024]{1,0:T(8,128)(2,1)S(1)}, bf16[256,1024]{1,0:T(8,128)(2,1)S(1)}, u32[]{:S(2)}, u32[]{:S(2)}) collective-permute-start(bf16[256,1024]{1,0:T(8,128)(2,1)S(1)} %shard_map.89.refs_4_.wo), channel_id=1, source_target_pairs={{0,4},{1,5},{2,6},{3,7},{4,8},{5,9},{6,10},{7,11},{8,12},{9,13},{1... | collective-permute-start | bytes 1572872 | tf_op jit(solution)/shard_map/ppermute | solution.py:158
  5.6 32.4 %collective-permute-start = (bf16[448,1024]{1,0:T(8,128)(2,1)}, bf16[448,1024]{1,0:T(8,128)(2,1)S(1)}, u32[]{:S(2)}, u32[]{:S(2)}) collective-permute-start(bf16[448,1024]{1,0:T(8,128)(2,1)} %f0.7), channel_id=1, source_target_pairs={{0,1},{1,0},{2,3},{3,2},{4,5},{5,4},{6,7},{7,6},{8,9},{9,8},{10,11... | collective-permute-start | bytes 2752520 | tf_op jit(solution)/shard_map/ppermute | solution.py:161
  5.6 1.2 copy-start.4
  6.8 32.2 %copy-start.2 = (bf16[448,1024]{1,0:T(8,128)(2,1)S(1)}, bf16[448,1024]{1,0:T(8,128)(2,1)}, u32[]{:S(2)}) copy-start(bf16[448,1024]{1,0:T(8,128)(2,1)} %f0.7) | copy-start | bytes 2752516
  6.8 25.1 %collective-permute-start.2 = (bf16[1024,256]{1,0:T(8,128)(2,1)S(1)}, bf16[1024,256]{1,0:T(8,128)(2,1)S(1)}, u32[]{:S(2)}, u32[]{:S(2)}) collective-permute-start(bf16[1024,256]{1,0:T(8,128)(2,1)S(1)} %shard_map.84.wi.refs_4_), channel_id=1, source_target_pairs={{0,4},{1,5},{2,6},{3,7},{4,8},{5,9},{6,10},{7,11},{8,12},{9,13},{1... | collective-permute-start | bytes 1572872 | tf_op jit(solution)/shard_map/ppermute | solution.py:158
  21.4 19.3 %collective-permute-start.1 = (bf16[1024,256]{1,0:T(8,128)(2,1)S(1)}, bf16[1024,256]{1,0:T(8,128)(2,1)S(1)}, u32[]{:S(2)}, u32[]{:S(2)}) collective-permute-start(bf16[1024,256]{1,0:T(8,128)(2,1)S(1)} %shard_map.84.wi.refs_4_), channel_id=1, source_target_pairs={{0,2},{1,3},{2,8},{3,9},{4,6},{5,7},{6,12},{7,13},{8,10},{9,11},{1... | collective-permute-start | bytes 1572872 | tf_op jit(solution)/shard_map/ppermute | solution.py:158
  32.0 17.5 %collective-permute-start.4 = (bf16[256,1024]{1,0:T(8,128)(2,1)S(1)}, bf16[256,1024]{1,0:T(8,128)(2,1)S(1)}, u32[]{:S(2)}, u32[]{:S(2)}) collective-permute-start(bf16[256,1024]{1,0:T(8,128)(2,1)S(1)} %shard_map.89.refs_4_.wo), channel_id=1, source_target_pairs={{0,2},{1,3},{2,8},{3,9},{4,6},{5,7},{6,12},{7,13},{8,10},{9,11},{1... | collective-permute-start | bytes 1572872 | tf_op jit(solution)/shard_map/ppermute | solution.py:158
  34.3 45.8 %collective-permute-start.6 = (bf16[256,1024]{1,0:T(8,128)(2,1)S(1)}, bf16[256,1024]{1,0:T(8,128)(2,1)S(1)}, u32[]{:S(2)}, u32[]{:S(2)}) collective-permute-start(bf16[256,1024]{1,0:T(8,128)(2,1)S(1)} %collective-permute-done.5.refs_6_.wo), channel_id=1, source_target_pairs={{0,2},{1,3},{2,0},{3,1},{4,6},{5,7},{6,4},{7,5},{8,10},{9,11},{10,... | collective-permute-start | bytes 1572872 | tf_op jit(solution)/shard_map/ppermute | solution.py:158
  34.3 36.2 %collective-permute-start.3 = (bf16[1024,256]{1,0:T(8,128)(2,1)S(1)}, bf16[1024,256]{1,0:T(8,128)(2,1)S(1)}, u32[]{:S(2)}, u32[]{:S(2)}) collective-permute-start(bf16[1024,256]{1,0:T(8,128)(2,1)S(1)} %collective-permute-done.2.wi.refs_6_), channel_id=1, source_target_pairs={{0,2},{1,3},{2,0},{3,1},{4,6},{5,7},{6,4},{7,5},{8,10},{9,11},{10,... | collective-permute-start | bytes 1572872 | tf_op jit(solution)/shard_map/ppermute | solution.py:158
  38.0 68.7 %collective-permute-start.17 = (bf16[256,1024]{1,0:T(8,128)(2,1)S(1)}, bf16[256,1024]{1,0:T(8,128)(2,1)S(1)}, u32[]{:S(2)}, u32[]{:S(2)}) collective-permute-start(bf16[256,1024]{1,0:T(8,128)(2,1)S(1)} %get-tuple-element.49), channel_id=1, source_target_pairs={{4,0},{5,1},{6,2},{7,3},{8,4},{9,5},{10,6},{11,7},{12,8},{13,9},{1... | collective-permute-start | bytes 1572872 | tf_op jit(solution)/shard_map/ppermute | solution.py:158
  72.2 22.1 %collective-permute-start.15 = (bf16[256,1024]{1,0:T(8,128)(2,1)S(1)}, bf16[256,1024]{1,0:T(8,128)(2,1)S(1)}, u32[]{:S(2)}, u32[]{:S(2)}) collective-permute-start(bf16[256,1024]{1,0:T(8,128)(2,1)S(1)} %get-tuple-element.48), channel_id=1, source_target_pairs={{28,0},{29,1},{6,2},{7,3},{0,4},{1,5},{10,6},{11,7},{4,8},{5,9},{1... | collective-permute-start | bytes 1572872 | tf_op jit(solution)/shard_map/ppermute | solution.py:158
  81.4 24.1 %collective-permute-start.11 = (bf16[256,1024]{1,0:T(8,128)(2,1)S(1)}, bf16[256,1024]{1,0:T(8,128)(2,1)S(1)}, u32[]{:S(2)}, u32[]{:S(2)}) collective-permute-start(bf16[256,1024]{1,0:T(8,128)(2,1)S(1)} %get-tuple-element.42), channel_id=1, source_target_pairs={{28,0},{29,1},{6,2},{7,3},{0,4},{1,5},{10,6},{11,7},{4,8},{5,9},{1... | collective-permute-start | bytes 1572872 | tf_op jit(solution)/shard_map/ppermute | solution.py:158
  84.4 44.1 %collective-permute-start.7 = (bf16[448,1024]{1,0:T(8,128)(2,1)S(1)}, bf16[448,1024]{1,0:T(8,128)(2,1)S(1)}, u32[]{:S(2)}, u32[]{:S(2)}) collective-permute-start(bf16[448,1024]{1,0:T(8,128)(2,1)S(1)} %get-tuple-element.29), channel_id=1, source_target_pairs={{0,1},{1,0},{2,3},{3,2},{4,5},{5,4},{6,7},{7,6},{8,9},{9,8},{10,11... | collective-permute-start | bytes 2752520 | tf_op jit(solution)/shard_map/ppermute | solution.py:161
  86.6 43.1 %collective-permute-start.10 = (bf16[448,1024]{1,0:T(8,128)(2,1)S(1)}, bf16[448,1024]{1,0:T(8,128)(2,1)S(1)}, u32[]{:S(2)}, u32[]{:S(2)}) collective-permute-start(bf16[448,1024]{1,0:T(8,128)(2,1)S(1)} %get-tuple-element.39), channel_id=1, source_target_pairs={{0,1},{1,0},{2,3},{3,2},{4,5},{5,4},{6,7},{7,6},{8,9},{9,8},{10,11... | collective-permute-start | bytes 2752520 | tf_op jit(solution)/shard_map/ppermute | solution.py:161
  94.4 12.7 %collective-permute-start.16 = (bf16[256,1024]{1,0:T(8,128)(2,1)S(1)}, bf16[256,1024]{1,0:T(8,128)(2,1)S(1)}, u32[]{:S(2)}, u32[]{:S(2)}) collective-permute-start(bf16[256,1024]{1,0:T(8,128)(2,1)S(1)} %shard_map.105), channel_id=1, source_target_pairs={{2,0},{3,1},{8,2},{9,3},{6,4},{7,5},{12,6},{13,7},{10,8},{11,9},{1... | collective-permute-start | bytes 1572872 | tf_op jit(solution)/shard_map/ppermute | solution.py:158
  105.5 13.3 %collective-permute-start.13 = (bf16[256,1024]{1,0:T(8,128)(2,1)S(1)}, bf16[256,1024]{1,0:T(8,128)(2,1)S(1)}, u32[]{:S(2)}, u32[]{:S(2)}) collective-permute-start(bf16[256,1024]{1,0:T(8,128)(2,1)S(1)} %get-tuple-element.43), channel_id=1, source_target_pairs={{4,0},{5,1},{6,2},{7,3},{8,4},{9,5},{10,6},{11,7},{12,8},{13,9},{1... | collective-permute-start | bytes 1572872 | tf_op jit(solution)/shard_map/ppermute | solution.py:158
  106.7 21.6 %collective-permute-start.12 = (bf16[256,1024]{1,0:T(8,128)(2,1)S(1)}, bf16[256,1024]{1,0:T(8,128)(2,1)S(1)}, u32[]{:S(2)}, u32[]{:S(2)}) collective-permute-start(bf16[256,1024]{1,0:T(8,128)(2,1)S(1)} %shard_map.102), channel_id=1, source_target_pairs={{2,0},{3,1},{8,2},{9,3},{6,4},{7,5},{12,6},{13,7},{10,8},{11,9},{1... | collective-permute-start | bytes 1572872 | tf_op jit(solution)/shard_map/ppermute | solution.py:158
  107.2 23.5 %collective-permute-start.18 = (bf16[256,512]{1,0:T(8,128)(2,1)S(1)}, bf16[256,512]{1,0:T(8,128)(2,1)S(1)}, u32[]{:S(2)}, u32[]{:S(2)}) collective-permute-start(bf16[256,512]{1,0:T(8,128)(2,1)S(1)} %get-tuple-element.51), channel_id=1, source_target_pairs={{0,1},{1,0},{2,3},{3,2},{4,5},{5,4},{6,7},{7,6},{8,9},{9,8},{10,11... | collective-permute-start | bytes 786440 | tf_op jit(solution)/shard_map/ppermute | solution.py:161
  128.4 3.3 %collective-permute-start.14 = (bf16[256,512]{1,0:T(8,128)(2,1)S(1)}, bf16[256,512]{1,0:T(8,128)(2,1)S(1)}, u32[]{:S(2)}, u32[]{:S(2)}) collective-permute-start(bf16[256,512]{1,0:T(8,128)(2,1)S(1)} %get-tuple-element.45), channel_id=1, source_target_pairs={{0,1},{1,0},{2,3},{3,2},{4,5},{5,4},{6,7},{7,6},{8,9},{9,8},{10,11... | collective-permute-start | bytes 786440 | tf_op jit(solution)/shard_map/ppermute | solution.py:161
